TPU v7x, 32 devices: a whole 2x2x4 slice. The times are simulated.
32 devices in a mesh: pass: 8 (over z, x), cell: 4 (over y, core).
Axes of the slice: x: 2, y: 2, z: 4, core: 2. Of those that a mesh axis runs over, the one named last changes fastest.
Arguments:
- flow_state: float32 [2048, 4096], P('pass', 'cell'), may hold values from -6 to 6
- face_weights: float32 [4, 2048, 4096], P(None, 'pass', 'cell'), may hold values from 0.02 to 0.24
- forcing: float32 [2048, 4096], P('pass', 'cell'), may hold values from -1.2 to 1.2
- lagged_planes: float32 [8, 8, 4096], P('pass', None, 'cell'), may hold values from -6 to 6
- phase_lag: int32 [4, 2], replicated, may hold values from 0 to 8
- face_map: int32 [8, 4096], P('pass', 'cell'), may hold values from 0 to 4095, as said below
- surface_record: bfloat16 [8, 120, 4096], P('pass', None, 'cell'), may hold values from -6 to 6
- face_radius: float32 [2, 4096], P(None, 'cell'), may hold values from 0.3 to 1
- face_angle: float32 [2, 4096], P(None, 'cell'), may hold values from -0.3 to 0.3
- face_axial: float32 [2, 4096], P(None, 'cell'), may hold values from -0.3 to 0.3
- face_stagger: float32 [2, 4096], P(None, 'cell'), may hold values from -1.2 to 1.2
- face_area: float32 [2, 4096], P(None, 'cell'), may hold values from 0.5 to 1.5
- listeners: float32 [3, 1024], replicated, as said below
- observer_group: int32 [1024], replicated, may hold values from 0 to 15
Outputs:
- final_field: float32 [2048, 4096], P('pass', 'cell')
- acoustic: float32 [1024, 128], P('cell')
- array_signal: float32 [16, 128], replicated
Inputs may be any that keep to these rules, and one draw needn't show every extreme that they name: face_map[j, a] lies in the aligned block of 1024 axial indices that holds a, and for each j the entries of a block are a permutation of that block. `listeners`: every observer is between 1.3 and 4 from the anchor.
All inputs are finite; a program needn't handle non-finite values.
Results may differ from a plain program's by a relative error of at most 0.0035.
Values sent between devices are 32-bit elements; how exact they have to be, the bound alone decides.
A program may use at most 64 MiB of HBM per device.

v0:
```python
import math
import jax
import jax.numpy as jnp
from jax import lax
from jax.sharding import PartitionSpec as P

STEPS = 8
GROUPS = 16
sound_speed = 2.0


def padded(shard, sides, width):
    for axis, dim in sides:
        devices, length = (lax.axis_size(axis), shard.shape[dim])
        up = [(i, (i + 1) % devices) for i in range(devices - 1)]
        down = [(j, i) for i, j in up]
        last = lax.slice_in_dim(shard, length - width, length, axis=dim)
        initial = lax.slice_in_dim(shard, 0, width, axis=dim)
        before = lax.ppermute(last, axis, up)
        after = lax.ppermute(initial, axis, down)
        shard = jnp.concatenate([before, shard, after], axis=dim)
    return shard


def shifted(block, axis, distance):
    devices = range(lax.axis_size(axis))
    route = [((i - distance) % len(devices), i) for i in devices]
    return lax.ppermute(block, axis, route)


def relax(field, coeff, forcing, ghost_low, ghost_high):
    edges = jnp.stack([field[:, 0], field[:, -1]], axis=0)
    rim = padded(edges, (("cell", 0),), 1)
    below = jnp.concatenate([ghost_low[None, :], field[:-1, :]], axis=0)
    above = jnp.concatenate([field[1:, :], ghost_high[None, :]], axis=0)
    left = jnp.concatenate([rim[0][:, None], field[:, :-1]], axis=1)
    right = jnp.concatenate([field[:, 1:], rim[3][:, None]], axis=1)
    keep = 1.0 - coeff[0] - coeff[1] - coeff[2] - coeff[3]
    return (
        keep * field
        + coeff[0] * below
        + coeff[1] * above
        + coeff[2] * left
        + coeff[3] * right
        + forcing
    )


def time_rate(signal, axis):
    values = signal.astype(jnp.float32)
    length = values.shape[axis]
    inner = (
        lax.slice_in_dim(values, 2, length, axis=axis)
        - lax.slice_in_dim(values, 0, length - 2, axis=axis)
    ) * 0.5
    head = lax.slice_in_dim(values, 1, 2, axis=axis) - lax.slice_in_dim(values, 0, 1, axis=axis)
    tail = lax.slice_in_dim(values, length - 1, length, axis=axis) - lax.slice_in_dim(
        values, length - 2, length - 1, axis=axis
    )
    return jnp.concatenate([head, inner, tail], axis=axis).astype(jnp.bfloat16)


def kernel_pair(points, theta, radius, angle, axial, stagger, area, scale):
    phase = theta + angle
    cos_phase = jnp.cos(phase)
    sin_phase = jnp.sin(phase)
    normal_x = -jnp.cos(stagger) * sin_phase
    normal_y = jnp.cos(stagger) * cos_phase
    normal_z = jnp.sin(stagger)
    delta_x = points[0][:, None] - (radius * cos_phase)[None, :]
    delta_y = points[1][:, None] - (radius * sin_phase)[None, :]
    delta_z = points[2][:, None] - axial[None, :]
    dist_sq = delta_x * delta_x + delta_y * delta_y + delta_z * delta_z
    dist = jnp.sqrt(dist_sq)
    cosine = (
        normal_x[None, :] * delta_x + normal_y[None, :] * delta_y + normal_z[None, :] * delta_z
    ) / dist
    weight = (area * scale / (4.0 * math.pi))[None, :] * cosine
    press = (weight / dist_sq).astype(jnp.bfloat16)
    change = (weight / (sound_speed * dist)).astype(jnp.bfloat16)
    return jnp.concatenate([press, change], axis=1)


def on_device(
    flow_state,
    face_weights,
    forcing,
    lagged_planes,
    phase_lag,
    face_map,
    surface_record,
    face_radius,
    face_angle,
    face_axial,
    face_stagger,
    face_area,
    listeners,
    observer_group,
):
    passes = lax.axis_size("pass")
    cells = lax.axis_size("cell")
    pass_index = lax.axis_index("pass")
    cell_index = lax.axis_index("cell")
    passage_count = passes // 2
    half = pass_index % 2
    passage = pass_index // 2
    field = flow_state
    height = field.shape[0]
    width = field.shape[1]
    lower_levels = jnp.concatenate([field[None, 0, :], lagged_planes[0]], axis=0)
    upper_levels = jnp.concatenate([field[None, -1, :], lagged_planes[0]], axis=0)
    local_map = face_map[0] - cell_index * width
    after_lag = phase_lag[(passage + 1) % passage_count, 0]
    before_lag = phase_lag[(passage + passage_count - 1) % passage_count, 1]
    surfaces = []
    for level in range(STEPS):
        up_pick = jnp.where(half == 1, after_lag, 0)
        down_pick = jnp.where(half == 0, before_lag, 0)
        raw_low = shifted(upper_levels[up_pick], "pass", 1)
        raw_high = shifted(lower_levels[down_pick], "pass", -1)
        mapped = jnp.take(jnp.where(half == 0, raw_low, raw_high), local_map)
        ghost_low = jnp.where(half == 0, mapped, raw_low)
        ghost_high = jnp.where(half == 1, mapped, raw_high)
        field = relax(field, face_weights, forcing, ghost_low, ghost_high)
        lower_levels = jnp.concatenate([field[None, 0, :], lower_levels[:-1]], axis=0)
        upper_levels = jnp.concatenate([field[None, -1, :], upper_levels[:-1]], axis=0)
        surfaces.append(field[height // 2].astype(jnp.bfloat16))
    surface = jnp.concatenate([surface_record[0], jnp.stack(surfaces, axis=0)], axis=0)
    rate = time_rate(surface, 0)
    data = jnp.concatenate([surface, rate], axis=1)
    theta = passage.astype(jnp.float32) * (2.0 * math.pi / passage_count)
    scale = 64.0 / math.sqrt(width * cells * passes)
    radius = face_radius[half]
    angle = face_angle[half]
    axial = face_axial[half]
    stagger = face_stagger[half]
    area = face_area[half]
    per_cell = listeners.shape[1] // cells
    block = math.gcd(per_cell * lax.axis_size("cell"), 256)

    def one_block(offset):
        rows = offset * block + jnp.arange(block, dtype=jnp.int32)
        points = jnp.take(listeners, rows, axis=1)
        kernel = kernel_pair(points, theta, radius, angle, axial, stagger, area, scale)
        return lax.dot_general(
            kernel, data, (((1,), (1,)), ((), ())), preferred_element_type=jnp.float32
        )

    blocks = lax.map(
        one_block, jnp.arange(per_cell * lax.axis_size("cell") // block, dtype=jnp.int32)
    )
    share = lax.psum_scatter(
        blocks.reshape(per_cell * lax.axis_size("cell"), blocks.shape[-1]),
        "cell",
        scatter_dimension=0,
        tiled=True,
    )
    acoustic = lax.psum(share, "pass")
    labels = jnp.arange(GROUPS, dtype=jnp.int32)
    my_groups = lax.dynamic_slice_in_dim(observer_group, cell_index * per_cell, per_cell)
    member = (my_groups[None, :] == labels[:, None]).astype(jnp.float32)
    counts = jnp.sum((observer_group[None, :] == labels[:, None]).astype(jnp.float32), axis=1)
    partial_totals = jnp.dot(
        member, acoustic, precision=lax.Precision.HIGHEST, preferred_element_type=jnp.float32
    )
    totals = lax.psum(partial_totals, "cell")
    array_signal = totals / jnp.maximum(counts, 1.0)[:, None]
    return (field, acoustic, array_signal)


def solution(mesh):
    return jax.shard_map(
        on_device,
        mesh=mesh,
        in_specs=(
            P("pass", "cell"),
            P(None, "pass", "cell"),
            P("pass", "cell"),
            P("pass", None, "cell"),
            P(),
            P("pass", "cell"),
            P("pass", None, "cell"),
            P(None, "cell"),
            P(None, "cell"),
            P(None, "cell"),
            P(None, "cell"),
            P(None, "cell"),
            P(),
            P(),
        ),
        out_specs=(P("pass", "cell"), P("cell", None), P()),
        check_vma=False,
    )
```

profile of v0, /device:TPU:0, one launch (start us, length us, event | category | flops | bytes accessed | tf_op | source)
XLA Modules:
  0.0 348.3 jit_solution(7912482702422968674)
XLA Ops:
  8.5 2.4 collective-permute-start.2
  16.5 2.4 collective-permute-start
  18.9 3.1 collective-permute-start.1
  22.1 3.2 fusion.109
  25.3 1.7 fusion.108
  28.6 4.5 %gather_fusion.1 = f32[1024]{0:T(1024)S(1)} fusion(f32[1024]{0:T(1024)S(1)} %broadcast_select_fusion.7, s32[1024]{0:T(1024)S(1)} %fusion.82), kind=kCustom, calls=%fused_computation.clone | custom fusion | bytes 12288 | tf_op jit(solution)/shard_map/jit(_take)/gather | solution.py:121
  33.2 5.1 %fusion.22 = (f32[256,1024]{1,0:T(8,128)S(1)}, f32[256,1024]{1,0:T(8,128)S(1)}) fusion(f32[256,1024]{1,0:T(8,128)S(1)} %copy-done, f32[255,1024]{1,0:T(8,128)} %get-tuple-element.332, f32[1,1024]{1,0:T(1,128)S(1)} %bitcast.169, f32[1,1024]{1,0:T(1,128)S(1)} %bitcast.172, f32[255,1024]{1,0:T(8,128)} %get-tuple-element.331, ...), kind=kLoop, calls=%fused_computation.51 | loop fusion | flops 4718592 | bytes 12582912 | tf_op jit(solution)/shard_map/add | solution.py:40
  40.0 4.0 %collective-permute-start.6 = (f32[1,256]{1,0:T(1,128)S(1)}, f32[1,256]{1,0:T(1,128)S(1)}, u32[]{:S(2)}, u32[]{:S(2)}) collective-permute-start(f32[1,256]{1,0:T(1,128)S(1)} %bitcast.206), channel_id=1, source_target_pairs={{0,1},{1,2},{2,3},{4,5},{5,6},{6,7},{8,9},{9,10},{10,11},{12,13},{... | collective-permute-start | bytes 3080 | tf_op jit(solution)/shard_map/ppermute | solution.py:19
  45.5 4.7 %collective-permute-start.5 = (f32[1024]{0:T(1024)S(1)}, f32[1024]{0:T(1024)S(1)}, u32[]{:S(2)}, u32[]{:S(2)}) collective-permute-start(f32[1024]{0:T(1024)S(1)} %bitcast.189), channel_id=1, source_target_pairs={{4,0},{8,4},{12,8},{16,12},{20,16},{24,20},{28,24},{0,28},{5,1},{9... | collective-permute-start | bytes 12296 | tf_op jit(solution)/shard_map/ppermute | solution.py:28
  50.2 1.7 fusion.105
  52.2 4.5 %gather_fusion.2 = f32[1024]{0:T(1024)S(1)} fusion(f32[1024]{0:T(1024)S(1)} %broadcast_select_fusion.6, s32[1024]{0:T(1024)S(1)} %fusion.82), kind=kCustom, calls=%fused_computation.2.clone | custom fusion | bytes 12288 | tf_op jit(solution)/shard_map/jit(_take)/gather | solution.py:121
  56.8 4.8 %fusion.27 = f32[256,1024]{1,0:T(8,128)S(1)} fusion(f32[256,1024]{1,0:T(8,128)S(1)} %copy-done, f32[255,1024]{1,0:T(8,128)} %get-tuple-element.326, f32[1,1024]{1,0:T(1,128)S(1)} %bitcast.174, f32[1,1024]{1,0:T(1,128)S(1)} %bitcast.173, f32[255,1024]{1,0:T(8,128)} %get-tuple-element.325, f32[256,1023]{1,0:T(8,128)} %get-tuple-element.324, ...), kind=kLoop, calls=%fused_computation.60 | loop fusion | flops 3670016 | bytes 12582912 | tf_op jit(solution)/shard_map/add | solution.py:40
  63.3 4.1 %collective-permute-start.10 = (f32[1,256]{1,0:T(1,128)S(1)}, f32[1,256]{1,0:T(1,128)S(1)}, u32[]{:S(2)}, u32[]{:S(2)}) collective-permute-start(f32[1,256]{1,0:T(1,128)S(1)} %bitcast.216), channel_id=1, source_target_pairs={{0,1},{1,2},{2,3},{4,5},{5,6},{6,7},{8,9},{9,10},{10,11},{12,13},{... | collective-permute-start | bytes 3080 | tf_op jit(solution)/shard_map/ppermute | solution.py:19
  68.8 4.8 %collective-permute-start.9 = (f32[1024]{0:T(1024)S(1)}, f32[1024]{0:T(1024)S(1)}, u32[]{:S(2)}, u32[]{:S(2)}) collective-permute-start(f32[1024]{0:T(1024)S(1)} %bitcast.198), channel_id=1, source_target_pairs={{4,0},{8,4},{12,8},{16,12},{20,16},{24,20},{28,24},{0,28},{5,1},{9... | collective-permute-start | bytes 12296 | tf_op jit(solution)/shard_map/ppermute | solution.py:28
  75.6 4.5 %gather_fusion.3 = f32[1024]{0:T(1024)S(1)} fusion(f32[1024]{0:T(1024)S(1)} %broadcast_select_fusion.5, s32[1024]{0:T(1024)S(1)} %fusion.82), kind=kCustom, calls=%fused_computation.3.clone | custom fusion | bytes 12288 | tf_op jit(solution)/shard_map/jit(_take)/gather | solution.py:121
  80.1 5.1 %fusion.32 = f32[256,1024]{1,0:T(8,128)S(1)} fusion(f32[256,1024]{1,0:T(8,128)S(1)} %copy-done, f32[255,1024]{1,0:T(8,128)} %get-tuple-element.320, f32[1,1024]{1,0:T(1,128)S(1)} %bitcast.176, f32[1,1024]{1,0:T(1,128)S(1)} %bitcast.175, f32[255,1024]{1,0:T(8,128)} %get-tuple-element.319, f32[256,1023]{1,0:T(8,128)} %get-tuple-element.318, ...), kind=kLoop, calls=%fused_computation.69 | loop fusion | flops 3670016 | bytes 12582912 | tf_op jit(solution)/shard_map/add | solution.py:40
  86.9 4.3 %collective-permute-start.14 = (f32[1,256]{1,0:T(1,128)S(1)}, f32[1,256]{1,0:T(1,128)S(1)}, u32[]{:S(2)}, u32[]{:S(2)}) collective-permute-start(f32[1,256]{1,0:T(1,128)S(1)} %bitcast.205), channel_id=1, source_target_pairs={{0,1},{1,2},{2,3},{4,5},{5,6},{6,7},{8,9},{9,10},{10,11},{12,13},{... | collective-permute-start | bytes 3080 | tf_op jit(solution)/shard_map/ppermute | solution.py:19
  92.6 4.7 %collective-permute-start.13 = (f32[1024]{0:T(1024)S(1)}, f32[1024]{0:T(1024)S(1)}, u32[]{:S(2)}, u32[]{:S(2)}) collective-permute-start(f32[1024]{0:T(1024)S(1)} %bitcast.190), channel_id=1, source_target_pairs={{4,0},{8,4},{12,8},{16,12},{20,16},{24,20},{28,24},{0,28},{5,1},{9... | collective-permute-start | bytes 12296 | tf_op jit(solution)/shard_map/ppermute | solution.py:28
  97.3 1.7 fusion.99
  99.4 4.5 %gather_fusion.4 = f32[1024]{0:T(1024)S(1)} fusion(f32[1024]{0:T(1024)S(1)} %broadcast_select_fusion.4, s32[1024]{0:T(1024)S(1)} %fusion.82), kind=kCustom, calls=%fused_computation.4.clone | custom fusion | bytes 12288 | tf_op jit(solution)/shard_map/jit(_take)/gather | solution.py:121
  103.9 4.8 %fusion.37 = f32[256,1024]{1,0:T(8,128)S(1)} fusion(f32[256,1024]{1,0:T(8,128)S(1)} %copy-done, f32[255,1024]{1,0:T(8,128)} %get-tuple-element.314, f32[1,1024]{1,0:T(1,128)S(1)} %bitcast.178, f32[1,1024]{1,0:T(1,128)S(1)} %bitcast.177, f32[255,1024]{1,0:T(8,128)} %get-tuple-element.313, f32[256,1023]{1,0:T(8,128)} %get-tuple-element.312, ...), kind=kLoop, calls=%fused_computation.78 | loop fusion | flops 3670016 | bytes 12582912 | tf_op jit(solution)/shard_map/add | solution.py:40
  110.4 4.4 %collective-permute-start.18 = (f32[1,256]{1,0:T(1,128)S(1)}, f32[1,256]{1,0:T(1,128)S(1)}, u32[]{:S(2)}, u32[]{:S(2)}) collective-permute-start(f32[1,256]{1,0:T(1,128)S(1)} %bitcast.217), channel_id=1, source_target_pairs={{0,1},{1,2},{2,3},{4,5},{5,6},{6,7},{8,9},{9,10},{10,11},{12,13},{... | collective-permute-start | bytes 3080 | tf_op jit(solution)/shard_map/ppermute | solution.py:19
  116.2 4.8 %collective-permute-start.17 = (f32[1024]{0:T(1024)S(1)}, f32[1024]{0:T(1024)S(1)}, u32[]{:S(2)}, u32[]{:S(2)}) collective-permute-start(f32[1024]{0:T(1024)S(1)} %bitcast.199), channel_id=1, source_target_pairs={{4,0},{8,4},{12,8},{16,12},{20,16},{24,20},{28,24},{0,28},{5,1},{9... | collective-permute-start | bytes 12296 | tf_op jit(solution)/shard_map/ppermute | solution.py:28
  123.0 4.5 %gather_fusion.5 = f32[1024]{0:T(1024)S(1)} fusion(f32[1024]{0:T(1024)S(1)} %broadcast_select_fusion.3, s32[1024]{0:T(1024)S(1)} %fusion.82), kind=kCustom, calls=%fused_computation.5.clone | custom fusion | bytes 12288 | tf_op jit(solution)/shard_map/jit(_take)/gather | solution.py:121
  127.5 5.1 %fusion.42 = f32[256,1024]{1,0:T(8,128)S(1)} fusion(f32[256,1024]{1,0:T(8,128)S(1)} %copy-done, f32[255,1024]{1,0:T(8,128)} %get-tuple-element.308, f32[1,1024]{1,0:T(1,128)S(1)} %bitcast.180, f32[1,1024]{1,0:T(1,128)S(1)} %bitcast.179, f32[255,1024]{1,0:T(8,128)} %get-tuple-element.307, f32[256,1023]{1,0:T(8,128)} %get-tuple-element.306, ...), kind=kLoop, calls=%fused_computation.87 | loop fusion | flops 3670016 | bytes 12582912 | tf_op jit(solution)/shard_map/add | solution.py:40
  134.3 4.2 %collective-permute-start.22 = (f32[1,256]{1,0:T(1,128)S(1)}, f32[1,256]{1,0:T(1,128)S(1)}, u32[]{:S(2)}, u32[]{:S(2)}) collective-permute-start(f32[1,256]{1,0:T(1,128)S(1)} %bitcast.207), channel_id=1, source_target_pairs={{0,1},{1,2},{2,3},{4,5},{5,6},{6,7},{8,9},{9,10},{10,11},{12,13},{... | collective-permute-start | bytes 3080 | tf_op jit(solution)/shard_map/ppermute | solution.py:19
  139.8 3.5 collective-permute-start.21
  143.4 1.7 fusion.93
  145.4 4.3 %collective-permute-done.20 = f32[1024]{0:T(1024)S(1)} collective-permute-done((f32[1024]{0:T(1024)S(1)}, f32[1024]{0:T(1024)S(1)}, u32[]{:S(2)}, u32[]{:S(2)}) %collective-permute-start.20) | collective-permute-done | bytes 4128 | tf_op jit(solution)/shard_map/ppermute | solution.py:28
  149.7 4.5 %gather_fusion.6 = f32[1024]{0:T(1024)S(1)} fusion(f32[1024]{0:T(1024)S(1)} %broadcast_select_fusion.2, s32[1024]{0:T(1024)S(1)} %fusion.82), kind=kCustom, calls=%fused_computation.6.clone | custom fusion | bytes 12288 | tf_op jit(solution)/shard_map/jit(_take)/gather | solution.py:121
  154.3 4.8 %fusion.47 = f32[256,1024]{1,0:T(8,128)S(1)} fusion(f32[256,1024]{1,0:T(8,128)S(1)} %copy-done, f32[255,1024]{1,0:T(8,128)} %get-tuple-element.302, f32[1,1024]{1,0:T(1,128)S(1)} %bitcast.182, f32[1,1024]{1,0:T(1,128)S(1)} %bitcast.181, f32[255,1024]{1,0:T(8,128)} %get-tuple-element.301, f32[256,1023]{1,0:T(8,128)} %get-tuple-element.300, ...), kind=kLoop, calls=%fused_computation.96 | loop fusion | flops 3670016 | bytes 12582912 | tf_op jit(solution)/shard_map/add | solution.py:40
  160.8 4.3 %collective-permute-start.26 = (f32[1,256]{1,0:T(1,128)S(1)}, f32[1,256]{1,0:T(1,128)S(1)}, u32[]{:S(2)}, u32[]{:S(2)}) collective-permute-start(f32[1,256]{1,0:T(1,128)S(1)} %bitcast.218), channel_id=1, source_target_pairs={{0,1},{1,2},{2,3},{4,5},{5,6},{6,7},{8,9},{9,10},{10,11},{12,13},{... | collective-permute-start | bytes 3080 | tf_op jit(solution)/shard_map/ppermute | solution.py:19
  166.5 4.8 %collective-permute-start.25 = (f32[1024]{0:T(1024)S(1)}, f32[1024]{0:T(1024)S(1)}, u32[]{:S(2)}, u32[]{:S(2)}) collective-permute-start(f32[1024]{0:T(1024)S(1)} %bitcast.200), channel_id=1, source_target_pairs={{4,0},{8,4},{12,8},{16,12},{20,16},{24,20},{28,24},{0,28},{5,1},{9... | collective-permute-start | bytes 12296 | tf_op jit(solution)/shard_map/ppermute | solution.py:28
  173.2 4.5 %gather_fusion.7 = f32[1024]{0:T(1024)S(1)} fusion(f32[1024]{0:T(1024)S(1)} %broadcast_select_fusion.1, s32[1024]{0:T(1024)S(1)} %fusion.82), kind=kCustom, calls=%fused_computation.7.clone | custom fusion | bytes 12288 | tf_op jit(solution)/shard_map/jit(_take)/gather | solution.py:121
  177.8 5.1 %fusion.52 = f32[256,1024]{1,0:T(8,128)S(1)} fusion(f32[256,1024]{1,0:T(8,128)S(1)} %copy-done, f32[255,1024]{1,0:T(8,128)} %get-tuple-element.296, f32[1,1024]{1,0:T(1,128)S(1)} %bitcast.184, f32[1,1024]{1,0:T(1,128)S(1)} %bitcast.183, f32[255,1024]{1,0:T(8,128)} %get-tuple-element.295, f32[256,1023]{1,0:T(8,128)} %get-tuple-element.294, ...), kind=kLoop, calls=%fused_computation.105 | loop fusion | flops 3670016 | bytes 12582912 | tf_op jit(solution)/shard_map/add | solution.py:40
  184.6 5.1 %collective-permute-start.30 = (f32[1,256]{1,0:T(1,128)S(1)}, f32[1,256]{1,0:T(1,128)S(1)}, u32[]{:S(2)}, u32[]{:S(2)}) collective-permute-start(f32[1,256]{1,0:T(1,128)S(1)} %bitcast.210), channel_id=1, source_target_pairs={{0,1},{1,2},{2,3},{4,5},{5,6},{6,7},{8,9},{9,10},{10,11},{12,13},{... | collective-permute-start | bytes 3080 | tf_op jit(solution)/shard_map/ppermute | solution.py:19
  191.2 4.7 %collective-permute-start.29 = (f32[1024]{0:T(1024)S(1)}, f32[1024]{0:T(1024)S(1)}, u32[]{:S(2)}, u32[]{:S(2)}) collective-permute-start(f32[1024]{0:T(1024)S(1)} %bitcast.188), channel_id=1, source_target_pairs={{4,0},{8,4},{12,8},{16,12},{20,16},{24,20},{28,24},{0,28},{5,1},{9... | collective-permute-start | bytes 12296 | tf_op jit(solution)/shard_map/ppermute | solution.py:28
  195.9 1.7 fusion.87
  197.9 4.5 %gather_fusion.8 = f32[1024]{0:T(1024)S(1)} fusion(f32[1024]{0:T(1024)S(1)} %broadcast_select_fusion, s32[1024]{0:T(1024)S(1)} %fusion.82), kind=kCustom, calls=%fused_computation.8.clone | custom fusion | bytes 12288 | tf_op jit(solution)/shard_map/jit(_take)/gather | solution.py:121
  202.4 4.8 %fusion.57 = f32[256,1024]{1,0:T(8,128)S(1)} fusion(f32[256,1024]{1,0:T(8,128)S(1)} %copy-done, f32[255,1024]{1,0:T(8,128)} %get-tuple-element.290, f32[1,1024]{1,0:T(1,128)S(1)} %bitcast.171, f32[1,1024]{1,0:T(1,128)S(1)} %bitcast.170, f32[255,1024]{1,0:T(8,128)} %get-tuple-element.289, f32[256,1023]{1,0:T(8,128)} %get-tuple-element.288, ...), kind=kLoop, calls=%fused_computation.114 | loop fusion | flops 3670016 | bytes 12582912 | tf_op jit(solution)/shard_map/add | solution.py:40
  209.5 23.1 %while.13 = (s32[]{:T(128)}, f32[4,256,128]{2,1,0:T(8,128)}, f32[1024]{0:T(1024)S(1)}, f32[1,1024]{1,0:T(1,128)S(1)}, f32[]{:T(128)}, /*index=5*/f32[1024]{0:T(1...) while((s32[]{:T(128)}, f32[4,256,128]{2,1,0:T(8,128)}, ...), condition=%wide.region_1.3_spmd, body=%wide.region_0.2_spmd.sunk | while | flops 141568512 | bytes 2851517 | solution.py:149
  211.0 1.8 gather_fusion
  216.7 1.8 gather_fusion
  222.5 1.8 gather_fusion
  228.3 1.8 gather_fusion
  232.9 25.6 %reduce-scatter.2.cloned.1.call-done = f32[256,128]{1,0:T(8,128)} async-done(((f32[1024,128]{1,0:T(8,128)}), f32[256,128]{1,0:T(8,128)}) %reduce-scatter.2.cloned.1.call-update) | async-done | bytes 131088 | tf_op jit(solution)/shard_map/reduce_scatter | solution.py:152
  258.5 73.9 %all-reduce.2.cloned.1.call-done = f32[256,128]{1,0:T(8,128)} async-done(((f32[256,128]{1,0:T(8,128)}), f32[256,128]{1,0:T(8,128)}) %all-reduce.2.cloned.1.call-update) | async-done | bytes 131088 | tf_op jit(solution)/shard_map/psum | solution.py:158
  333.5 5.8 %psum.15 = f32[16,128]{1,0:T(8,128)S(1)} all-reduce(f32[16,128]{1,0:T(8,128)S(1)} %fusion.66), channel_id=1, replica_groups=mesh['pass'=8,'cell'=4] {'cell'}, use_global_device_ids=true, to_apply=%region_4.6 | all-reduce | flops 2048 | bytes 16384 | tf_op jit(solution)/shard_map/psum | solution.py:166
  (228 shorter events, 54.9 us)
Async XLA Ops:
  7.2 18.1 %copy-start.4 = (f32[256,1024]{1,0:T(8,128)S(1)}, f32[256,1024]{1,0:T(8,128)}, u32[]{:S(2)}) copy-start(f32[256,1024]{1,0:T(8,128)} %param.18) | copy-start | bytes 3145732
  7.2 251.3 %reduce-scatter.2.cloned.1.call-start = ((), (), s32[]{:S(2)}) async-start(), calls=%async_computation.1 | async-start | bytes 655360 | tf_op jit(solution)/shard_map/reduce_scatter | solution.py:152
  8.5 20.0 %collective-permute-start.2 = (f32[1,256]{1,0:T(1,128)S(1)}, f32[1,256]{1,0:T(1,128)S(1)}, u32[]{:S(2)}, u32[]{:S(2)}) collective-permute-start(f32[1,256]{1,0:T(1,128)S(1)} %bitcast.202), channel_id=1, source_target_pairs={{0,1},{1,2},{2,3},{4,5},{5,6},{6,7},{8,9},{9,10},{10,11},{12,13},{... | collective-permute-start | bytes 3080 | tf_op jit(solution)/shard_map/ppermute | solution.py:19
  10.9 17.4 %collective-permute-start.3 = (f32[1,256]{1,0:T(1,128)S(1)}, f32[1,256]{1,0:T(1,128)S(1)}, u32[]{:S(2)}, u32[]{:S(2)}) collective-permute-start(f32[1,256]{1,0:T(1,128)S(1)} %bitcast.203), channel_id=1, source_target_pairs={{1,0},{2,1},{3,2},{5,4},{6,5},{7,6},{9,8},{10,9},{11,10},{13,12},{... | collective-permute-start | bytes 3080 | tf_op jit(solution)/shard_map/ppermute | solution.py:20
  16.5 12.0 %collective-permute-start = (f32[1024]{0:T(1024)S(1)}, f32[1024]{0:T(1024)S(1)}, u32[]{:S(2)}, u32[]{:S(2)}) collective-permute-start(f32[1024]{0:T(1024)S(1)} %bitcast.186), channel_id=1, source_target_pairs={{28,0},{0,4},{4,8},{8,12},{12,16},{16,20},{20,24},{24,28},{29,1},{... | collective-permute-start | bytes 12296 | tf_op jit(solution)/shard_map/ppermute | solution.py:28
  18.9 9.7 %collective-permute-start.1 = (f32[1024]{0:T(1024)S(1)}, f32[1024]{0:T(1024)S(1)}, u32[]{:S(2)}, u32[]{:S(2)}) collective-permute-start(f32[1024]{0:T(1024)S(1)} %bitcast.185), channel_id=1, source_target_pairs={{4,0},{8,4},{12,8},{16,12},{20,16},{24,20},{28,24},{0,28},{5,1},{9... | collective-permute-start | bytes 12296 | tf_op jit(solution)/shard_map/ppermute | solution.py:28
  22.0 5.0 %copy-start.9 = (s32[1,1024]{1,0:T(1,128)S(1)}, s32[1,1024]{1,0:T(1,128)}, u32[]{:S(2)}) copy-start(s32[1,1024]{1,0:T(1,128)} %param.23) | copy-start | bytes 12292
  22.0 5.0 %copy-start.10 = (f32[2,1024]{1,0:T(2,128)S(1)}, f32[2,1024]{1,0:T(2,128)}, u32[]{:S(2)}) copy-start(f32[2,1024]{1,0:T(2,128)} %param.28) | copy-start | bytes 24580
  22.0 5.1 %copy-start.11 = (f32[2,1024]{1,0:T(2,128)S(1)}, f32[2,1024]{1,0:T(2,128)}, u32[]{:S(2)}) copy-start(f32[2,1024]{1,0:T(2,128)} %param.27) | copy-start | bytes 24580
  22.0 5.1 %copy-start.12 = (f32[2,1024]{1,0:T(2,128)S(1)}, f32[2,1024]{1,0:T(2,128)}, u32[]{:S(2)}) copy-start(f32[2,1024]{1,0:T(2,128)} %param.25) | copy-start | bytes 24580
  22.0 5.2 %copy-start.13 = (f32[2,1024]{1,0:T(2,128)S(1)}, f32[2,1024]{1,0:T(2,128)}, u32[]{:S(2)}) copy-start(f32[2,1024]{1,0:T(2,128)} %param.26) | copy-start | bytes 24580
  22.0 5.2 %copy-start.14 = (f32[2,1024]{1,0:T(2,128)S(1)}, f32[2,1024]{1,0:T(2,128)}, u32[]{:S(2)}) copy-start(f32[2,1024]{1,0:T(2,128)} %param.29) | copy-start | bytes 24580
  22.0 5.2 %copy-start.7 = (f32[3,1024]{1,0:T(4,128)S(1)}, f32[3,1024]{1,0:T(4,128)}, u32[]{:S(2)}) copy-start(f32[3,1024]{1,0:T(4,128)} %param.30) | copy-start | bytes 36868
  25.3 7.9 %copy-start = (f32[256,1024]{1,0:T(8,128)S(1)}, f32[256,1024]{1,0:T(8,128)}, u32[]{:S(2)}) copy-start(f32[256,1024]{1,0:T(8,128)} %param.20) | copy-start | bytes 3145732
  38.3 7.1 %copy-start.6 = (f32[1,8,1024]{2,1,0:T(8,128)S(1)}, f32[1,8,1024]{2,1,0:T(8,128)}, u32[]{:S(2)}) copy-start(f32[1,8,1024]{2,1,0:T(8,128)} %param.21) | copy-start | bytes 98308
  40.0 12.1 %collective-permute-start.6 = (f32[1,256]{1,0:T(1,128)S(1)}, f32[1,256]{1,0:T(1,128)S(1)}, u32[]{:S(2)}, u32[]{:S(2)}) collective-permute-start(f32[1,256]{1,0:T(1,128)S(1)} %bitcast.206), channel_id=1, source_target_pairs={{0,1},{1,2},{2,3},{4,5},{5,6},{6,7},{8,9},{9,10},{10,11},{12,13},{... | collective-permute-start | bytes 3080 | tf_op jit(solution)/shard_map/ppermute | solution.py:19
  44.0 7.9 %collective-permute-start.7 = (f32[1,256]{1,0:T(1,128)S(1)}, f32[1,256]{1,0:T(1,128)S(1)}, u32[]{:S(2)}, u32[]{:S(2)}) collective-permute-start(f32[1,256]{1,0:T(1,128)S(1)} %bitcast.211), channel_id=1, source_target_pairs={{1,0},{2,1},{3,2},{5,4},{6,5},{7,6},{9,8},{10,9},{11,10},{13,12},{... | collective-permute-start | bytes 3080 | tf_op jit(solution)/shard_map/ppermute | solution.py:20
  45.4 6.8 %collective-permute-start.4 = (f32[1024]{0:T(1024)S(1)}, f32[1024]{0:T(1024)S(1)}, u32[]{:S(2)}, u32[]{:S(2)}) collective-permute-start(f32[1024]{0:T(1024)S(1)} %bitcast.192), channel_id=1, source_target_pairs={{28,0},{0,4},{4,8},{8,12},{12,16},{16,20},{20,24},{24,28},{29,1},{... | collective-permute-start | bytes 12296 | tf_op jit(solution)/shard_map/ppermute | solution.py:28
  45.5 6.7 %collective-permute-start.5 = (f32[1024]{0:T(1024)S(1)}, f32[1024]{0:T(1024)S(1)}, u32[]{:S(2)}, u32[]{:S(2)}) collective-permute-start(f32[1024]{0:T(1024)S(1)} %bitcast.189), channel_id=1, source_target_pairs={{4,0},{8,4},{12,8},{16,12},{20,16},{24,20},{28,24},{0,28},{5,1},{9... | collective-permute-start | bytes 12296 | tf_op jit(solution)/shard_map/ppermute | solution.py:28
  61.6 13.7 %copy-start.1 = (f32[256,1024]{1,0:T(8,128)}, f32[256,1024]{1,0:T(8,128)S(1)}, u32[]{:S(2)}) copy-start(f32[256,1024]{1,0:T(8,128)S(1)} %fusion.27) | copy-start | bytes 3145732
  63.3 12.1 %collective-permute-start.10 = (f32[1,256]{1,0:T(1,128)S(1)}, f32[1,256]{1,0:T(1,128)S(1)}, u32[]{:S(2)}, u32[]{:S(2)}) collective-permute-start(f32[1,256]{1,0:T(1,128)S(1)} %bitcast.216), channel_id=1, source_target_pairs={{0,1},{1,2},{2,3},{4,5},{5,6},{6,7},{8,9},{9,10},{10,11},{12,13},{... | collective-permute-start | bytes 3080 | tf_op jit(solution)/shard_map/ppermute | solution.py:19
  67.4 7.9 %collective-permute-start.11 = (f32[1,256]{1,0:T(1,128)S(1)}, f32[1,256]{1,0:T(1,128)S(1)}, u32[]{:S(2)}, u32[]{:S(2)}) collective-permute-start(f32[1,256]{1,0:T(1,128)S(1)} %bitcast.222), channel_id=1, source_target_pairs={{1,0},{2,1},{3,2},{5,4},{6,5},{7,6},{9,8},{10,9},{11,10},{13,12},{... | collective-permute-start | bytes 3080 | tf_op jit(solution)/shard_map/ppermute | solution.py:20
  68.7 6.8 %collective-permute-start.8 = (f32[1024]{0:T(1024)S(1)}, f32[1024]{0:T(1024)S(1)}, u32[]{:S(2)}, u32[]{:S(2)}) collective-permute-start(f32[1024]{0:T(1024)S(1)} %bitcast.195), channel_id=1, source_target_pairs={{28,0},{0,4},{4,8},{8,12},{12,16},{16,20},{20,24},{24,28},{29,1},{... | collective-permute-start | bytes 12296 | tf_op jit(solution)/shard_map/ppermute | solution.py:28
  68.8 6.7 %collective-permute-start.9 = (f32[1024]{0:T(1024)S(1)}, f32[1024]{0:T(1024)S(1)}, u32[]{:S(2)}, u32[]{:S(2)}) collective-permute-start(f32[1024]{0:T(1024)S(1)} %bitcast.198), channel_id=1, source_target_pairs={{4,0},{8,4},{12,8},{16,12},{20,16},{24,20},{28,24},{0,28},{5,1},{9... | collective-permute-start | bytes 12296 | tf_op jit(solution)/shard_map/ppermute | solution.py:28
  86.9 12.3 %collective-permute-start.14 = (f32[1,256]{1,0:T(1,128)S(1)}, f32[1,256]{1,0:T(1,128)S(1)}, u32[]{:S(2)}, u32[]{:S(2)}) collective-permute-start(f32[1,256]{1,0:T(1,128)S(1)} %bitcast.205), channel_id=1, source_target_pairs={{0,1},{1,2},{2,3},{4,5},{5,6},{6,7},{8,9},{9,10},{10,11},{12,13},{... | collective-permute-start | bytes 3080 | tf_op jit(solution)/shard_map/ppermute | solution.py:19
  91.2 7.9 %collective-permute-start.15 = (f32[1,256]{1,0:T(1,128)S(1)}, f32[1,256]{1,0:T(1,128)S(1)}, u32[]{:S(2)}, u32[]{:S(2)}) collective-permute-start(f32[1,256]{1,0:T(1,128)S(1)} %bitcast.208), channel_id=1, source_target_pairs={{1,0},{2,1},{3,2},{5,4},{6,5},{7,6},{9,8},{10,9},{11,10},{13,12},{... | collective-permute-start | bytes 3080 | tf_op jit(solution)/shard_map/ppermute | solution.py:20
  92.6 6.8 %collective-permute-start.12 = (f32[1024]{0:T(1024)S(1)}, f32[1024]{0:T(1024)S(1)}, u32[]{:S(2)}, u32[]{:S(2)}) collective-permute-start(f32[1024]{0:T(1024)S(1)} %bitcast.193), channel_id=1, source_target_pairs={{28,0},{0,4},{4,8},{8,12},{12,16},{16,20},{20,24},{24,28},{29,1},{... | collective-permute-start | bytes 12296 | tf_op jit(solution)/shard_map/ppermute | solution.py:28
  92.6 6.7 %collective-permute-start.13 = (f32[1024]{0:T(1024)S(1)}, f32[1024]{0:T(1024)S(1)}, u32[]{:S(2)}, u32[]{:S(2)}) collective-permute-start(f32[1024]{0:T(1024)S(1)} %bitcast.190), channel_id=1, source_target_pairs={{4,0},{8,4},{12,8},{16,12},{20,16},{24,20},{28,24},{0,28},{5,1},{9... | collective-permute-start | bytes 12296 | tf_op jit(solution)/shard_map/ppermute | solution.py:28
  108.7 13.9 %copy-start.2 = (f32[256,1024]{1,0:T(8,128)}, f32[256,1024]{1,0:T(8,128)S(1)}, u32[]{:S(2)}) copy-start(f32[256,1024]{1,0:T(8,128)S(1)} %fusion.37) | copy-start | bytes 3145732
  110.4 12.4 %collective-permute-start.18 = (f32[1,256]{1,0:T(1,128)S(1)}, f32[1,256]{1,0:T(1,128)S(1)}, u32[]{:S(2)}, u32[]{:S(2)}) collective-permute-start(f32[1,256]{1,0:T(1,128)S(1)} %bitcast.217), channel_id=1, source_target_pairs={{0,1},{1,2},{2,3},{4,5},{5,6},{6,7},{8,9},{9,10},{10,11},{12,13},{... | collective-permute-start | bytes 3080 | tf_op jit(solution)/shard_map/ppermute | solution.py:19
  114.8 7.9 %collective-permute-start.19 = (f32[1,256]{1,0:T(1,128)S(1)}, f32[1,256]{1,0:T(1,128)S(1)}, u32[]{:S(2)}, u32[]{:S(2)}) collective-permute-start(f32[1,256]{1,0:T(1,128)S(1)} %bitcast.224), channel_id=1, source_target_pairs={{1,0},{2,1},{3,2},{5,4},{6,5},{7,6},{9,8},{10,9},{11,10},{13,12},{... | collective-permute-start | bytes 3080 | tf_op jit(solution)/shard_map/ppermute | solution.py:20
  116.1 6.8 %collective-permute-start.16 = (f32[1024]{0:T(1024)S(1)}, f32[1024]{0:T(1024)S(1)}, u32[]{:S(2)}, u32[]{:S(2)}) collective-permute-start(f32[1024]{0:T(1024)S(1)} %bitcast.196), channel_id=1, source_target_pairs={{28,0},{0,4},{4,8},{8,12},{12,16},{16,20},{20,24},{24,28},{29,1},{... | collective-permute-start | bytes 12296 | tf_op jit(solution)/shard_map/ppermute | solution.py:28
  116.2 6.7 %collective-permute-start.17 = (f32[1024]{0:T(1024)S(1)}, f32[1024]{0:T(1024)S(1)}, u32[]{:S(2)}, u32[]{:S(2)}) collective-permute-start(f32[1024]{0:T(1024)S(1)} %bitcast.199), channel_id=1, source_target_pairs={{4,0},{8,4},{12,8},{16,12},{20,16},{24,20},{28,24},{0,28},{5,1},{9... | collective-permute-start | bytes 12296 | tf_op jit(solution)/shard_map/ppermute | solution.py:28
  134.3 11.0 %collective-permute-start.22 = (f32[1,256]{1,0:T(1,128)S(1)}, f32[1,256]{1,0:T(1,128)S(1)}, u32[]{:S(2)}, u32[]{:S(2)}) collective-permute-start(f32[1,256]{1,0:T(1,128)S(1)} %bitcast.207), channel_id=1, source_target_pairs={{0,1},{1,2},{2,3},{4,5},{5,6},{6,7},{8,9},{9,10},{10,11},{12,13},{... | collective-permute-start | bytes 3080 | tf_op jit(solution)/shard_map/ppermute | solution.py:19
  138.5 6.6 %collective-permute-start.23 = (f32[1,256]{1,0:T(1,128)S(1)}, f32[1,256]{1,0:T(1,128)S(1)}, u32[]{:S(2)}, u32[]{:S(2)}) collective-permute-start(f32[1,256]{1,0:T(1,128)S(1)} %bitcast.213), channel_id=1, source_target_pairs={{1,0},{2,1},{3,2},{5,4},{6,5},{7,6},{9,8},{10,9},{11,10},{13,12},{... | collective-permute-start | bytes 3080 | tf_op jit(solution)/shard_map/ppermute | solution.py:20
  139.8 5.6 %collective-permute-start.21 = (f32[1024]{0:T(1024)S(1)}, f32[1024]{0:T(1024)S(1)}, u32[]{:S(2)}, u32[]{:S(2)}) collective-permute-start(f32[1024]{0:T(1024)S(1)} %bitcast.191), channel_id=1, source_target_pairs={{4,0},{8,4},{12,8},{16,12},{20,16},{24,20},{28,24},{0,28},{5,1},{9... | collective-permute-start | bytes 12296 | tf_op jit(solution)/shard_map/ppermute | solution.py:28
  143.4 6.4 %collective-permute-start.20 = (f32[1024]{0:T(1024)S(1)}, f32[1024]{0:T(1024)S(1)}, u32[]{:S(2)}, u32[]{:S(2)}) collective-permute-start(f32[1024]{0:T(1024)S(1)} %bitcast.194), channel_id=1, source_target_pairs={{28,0},{0,4},{4,8},{8,12},{12,16},{16,20},{20,24},{24,28},{29,1},{... | collective-permute-start | bytes 12296 | tf_op jit(solution)/shard_map/ppermute | solution.py:28
  159.1 13.8 %copy-start.3 = (f32[256,1024]{1,0:T(8,128)}, f32[256,1024]{1,0:T(8,128)S(1)}, u32[]{:S(2)}) copy-start(f32[256,1024]{1,0:T(8,128)S(1)} %fusion.47) | copy-start | bytes 3145732
  160.8 12.3 %collective-permute-start.26 = (f32[1,256]{1,0:T(1,128)S(1)}, f32[1,256]{1,0:T(1,128)S(1)}, u32[]{:S(2)}, u32[]{:S(2)}) collective-permute-start(f32[1,256]{1,0:T(1,128)S(1)} %bitcast.218), channel_id=1, source_target_pairs={{0,1},{1,2},{2,3},{4,5},{5,6},{6,7},{8,9},{9,10},{10,11},{12,13},{... | collective-permute-start | bytes 3080 | tf_op jit(solution)/shard_map/ppermute | solution.py:19
  165.0 7.9 %collective-permute-start.27 = (f32[1,256]{1,0:T(1,128)S(1)}, f32[1,256]{1,0:T(1,128)S(1)}, u32[]{:S(2)}, u32[]{:S(2)}) collective-permute-start(f32[1,256]{1,0:T(1,128)S(1)} %bitcast.226), channel_id=1, source_target_pairs={{1,0},{2,1},{3,2},{5,4},{6,5},{7,6},{9,8},{10,9},{11,10},{13,12},{... | collective-permute-start | bytes 3080 | tf_op jit(solution)/shard_map/ppermute | solution.py:20
  166.4 6.8 %collective-permute-start.24 = (f32[1024]{0:T(1024)S(1)}, f32[1024]{0:T(1024)S(1)}, u32[]{:S(2)}, u32[]{:S(2)}) collective-permute-start(f32[1024]{0:T(1024)S(1)} %bitcast.197), channel_id=1, source_target_pairs={{28,0},{0,4},{4,8},{8,12},{12,16},{16,20},{20,24},{24,28},{29,1},{... | collective-permute-start | bytes 12296 | tf_op jit(solution)/shard_map/ppermute | solution.py:28
  166.5 6.7 %collective-permute-start.25 = (f32[1024]{0:T(1024)S(1)}, f32[1024]{0:T(1024)S(1)}, u32[]{:S(2)}, u32[]{:S(2)}) collective-permute-start(f32[1024]{0:T(1024)S(1)} %bitcast.200), channel_id=1, source_target_pairs={{4,0},{8,4},{12,8},{16,12},{20,16},{24,20},{28,24},{0,28},{5,1},{9... | collective-permute-start | bytes 12296 | tf_op jit(solution)/shard_map/ppermute | solution.py:28
  184.6 13.0 %collective-permute-start.30 = (f32[1,256]{1,0:T(1,128)S(1)}, f32[1,256]{1,0:T(1,128)S(1)}, u32[]{:S(2)}, u32[]{:S(2)}) collective-permute-start(f32[1,256]{1,0:T(1,128)S(1)} %bitcast.210), channel_id=1, source_target_pairs={{0,1},{1,2},{2,3},{4,5},{5,6},{6,7},{8,9},{9,10},{10,11},{12,13},{... | collective-permute-start | bytes 3080 | tf_op jit(solution)/shard_map/ppermute | solution.py:19
  189.8 7.7 %collective-permute-start.31 = (f32[1,256]{1,0:T(1,128)S(1)}, f32[1,256]{1,0:T(1,128)S(1)}, u32[]{:S(2)}, u32[]{:S(2)}) collective-permute-start(f32[1,256]{1,0:T(1,128)S(1)} %bitcast.215), channel_id=1, source_target_pairs={{1,0},{2,1},{3,2},{5,4},{6,5},{7,6},{9,8},{10,9},{11,10},{13,12},{... | collective-permute-start | bytes 3080 | tf_op jit(solution)/shard_map/ppermute | solution.py:20
  191.1 6.7 %collective-permute-start.28 = (f32[1024]{0:T(1024)S(1)}, f32[1024]{0:T(1024)S(1)}, u32[]{:S(2)}, u32[]{:S(2)}) collective-permute-start(f32[1024]{0:T(1024)S(1)} %bitcast.187), channel_id=1, source_target_pairs={{28,0},{0,4},{4,8},{8,12},{12,16},{16,20},{20,24},{24,28},{29,1},{... | collective-permute-start | bytes 12296 | tf_op jit(solution)/shard_map/ppermute | solution.py:28
  191.2 6.7 %collective-permute-start.29 = (f32[1024]{0:T(1024)S(1)}, f32[1024]{0:T(1024)S(1)}, u32[]{:S(2)}, u32[]{:S(2)}) collective-permute-start(f32[1024]{0:T(1024)S(1)} %bitcast.188), channel_id=1, source_target_pairs={{4,0},{8,4},{12,8},{16,12},{20,16},{24,20},{28,24},{0,28},{5,1},{9... | collective-permute-start | bytes 12296 | tf_op jit(solution)/shard_map/ppermute | solution.py:28
  209.5 23.2 %copy-start.8 = (s32[1024]{0:T(1024)S(1)}, s32[1024]{0:T(1024)}, u32[]{:S(2)}) copy-start(s32[1024]{0:T(1024)} %param.31) | copy-start | bytes 12292
  232.7 99.7 %all-reduce.2.cloned.1.call-start = ((), (), s32[]{:S(2)}) async-start(), calls=%async_computation.2 | async-start | bytes 262144 | tf_op jit(solution)/shard_map/psum | solution.py:158
  (1 other events, 1.0 us)
Sparse Core Ops, SparseCore 0:
  232.8 25.6 reduce-scatter.1
  261.8 70.4 all-reduce.1
where the time goes:
time: 349 us; the launch traced here: 348 us
  waiting for transfers between devices  104 us (30%)
  local copies, waits for them, and re-layouts  85.8 us (25%)
  starting transfers between devices  80.9 us (23%)
  other arithmetic  47.1 us (13%)
  between operations  16.7 us (5%)
  blocking collectives  5.77 us (2%)
  matrix products  5.43 us (2%)
    psum x1, waiting for transfers between devices, on_device(): acoustic = lax.psum(share, 'pass')  73.9 us
    add x8, other arithmetic, relax(): keep * field + coeff[0] * below + coeff[1] * above + coeff[2] * left  39.5 us
    ppermute x16, starting transfers between devices, shifted(): return lax.ppermute(block, axis, route)  37.7 us
    gather x8, local copies, waits for them, and re-layouts, on_device(): mapped = jnp.take(jnp.where(half == 0, raw_low, raw_high), local_map)  36.2 us
    ppermute x8, starting transfers between devices, padded(): before = lax.ppermute(last, axis, up)  32.7 us
    reduce_scatter x1, waiting for transfers between devices, on_device(): lax.psum_scatter(blocks.reshape(per_cell * lax.axis_size('cell'), blocks....  25.6 us
    slice x8, local copies, waits for them, and re-layouts, relax(): above = jnp.concatenate([field[1:, :], ghost_high[None, :]], axis=0)  13.6 us
    slice x8, local copies, waits for them, and re-layouts, relax(): right = jnp.concatenate([field[:, 1:], rim[3][:, None]], axis=1)  13.3 us
  transfers between devices with their start and end apart: 34, of which 3 were waited for; matrix products, arithmetic and copies ran while one was open for 7% of the time, Pallas kernels for 0%

commit v1 on v0

--- a/solution.py
+++ b/solution.py
@@ -3,6 +3,7 @@
 import jax.numpy as jnp
 from jax import lax
 from jax.sharding import PartitionSpec as P
+from jax.lax import axis_size, ppermute
 
 STEPS = 8
 GROUPS = 16
@@ -155,7 +156,14 @@
         scatter_dimension=0,
         tiled=True,
     )
-    acoustic = lax.psum(share, "pass")
+    num_devices = axis_size("pass")
+    acoustic, w_next = (share, 0)
+    while 1 << w_next < num_devices:
+        m_next = ppermute(
+            acoustic, "pass", [(dev_j, dev_j ^ 1 << w_next) for dev_j in range(num_devices)]
+        )
+        acoustic = acoustic + m_next
+        w_next = w_next + 1
     labels = jnp.arange(GROUPS, dtype=jnp.int32)
     my_groups = lax.dynamic_slice_in_dim(observer_group, cell_index * per_cell, per_cell)
     member = (my_groups[None, :] == labels[:, None]).astype(jnp.float32)

time: 349 us -> 292 us (0.84)
  waiting for transfers between devices: 104 us -> 42.3 us
  starting transfers between devices: 80.9 us -> 86.3 us
    psum x1 -> x0, waiting for transfers between devices: 73.9 us -> none  [on_device(): acoustic = lax.psum(share, 'pass')]
    ppermute x0 -> x3, waiting for transfers between devices: none -> 12 us  [on_device(): ppermute(acoustic, 'pass', [(dev_j, dev_j ^ 1 << w_next) for dev_j in ran...]
    ppermute x0 -> x3, starting transfers between devices: none -> 5.45 us  [on_device(): ppermute(acoustic, 'pass', [(dev_j, dev_j ^ 1 << w_next) for dev_j in ran...]
  transfers between devices with their start and end apart: 34 -> 36, of which waited for: 3 -> 5; matrix products, arithmetic and copies ran while one was open for 7% -> 8% of each run, Pallas kernels for 0% -> 0%
where the time goes in v1:
time: 292 us; the launch traced here: 291 us
  starting transfers between devices  86.3 us (30%)
  local copies, waits for them, and re-layouts  83.9 us (29%)
  other arithmetic  48 us (16%)
  waiting for transfers between devices  42.3 us (14%)
  between operations  16.7 us (6%)
  blocking collectives  6.06 us (2%)
  matrix products  4.57 us (2%)
    add x8, other arithmetic, relax(): keep * field + coeff[0] * below + coeff[1] * above + coeff[2] * left  39.5 us
    ppermute x16, starting transfers between devices, shifted(): return lax.ppermute(block, axis, route)  37.8 us
    gather x8, local copies, waits for them, and re-layouts, on_device(): mapped = jnp.take(jnp.where(half == 0, raw_low, raw_high), local_map)  36.2 us
    ppermute x8, starting transfers between devices, padded(): before = lax.ppermute(last, axis, up)  32.7 us
    reduce_scatter x1, waiting for transfers between devices, on_device(): lax.psum_scatter(blocks.reshape(per_cell * lax.axis_size('cell'), blocks....  25.9 us
    slice x8, local copies, waits for them, and re-layouts, relax(): above = jnp.concatenate([field[1:, :], ghost_high[None, :]], axis=0)  13.6 us
    slice x8, local copies, waits for them, and re-layouts, relax(): right = jnp.concatenate([field[:, 1:], rim[3][:, None]], axis=1)  13.2 us
    ppermute x3, waiting for transfers between devices, on_device(): ppermute(acoustic, 'pass', [(dev_j, dev_j ^ 1 << w_next) for dev_j in ran...  12 us
  transfers between devices with their start and end apart: 36, of which 5 were waited for; matrix products, arithmetic and copies ran while one was open for 8% of the time, Pallas kernels for 0%

profile of v1, /device:TPU:0, one launch (start us, length us, event | category | flops | bytes accessed | tf_op | source)
XLA Modules:
  0.0 290.5 jit_solution(13466452393940864646)
XLA Ops:
  8.5 2.4 collective-permute-start.2
  16.5 2.4 collective-permute-start
  18.9 3.1 %collective-permute-start.1 = (f32[1024]{0:T(1024)S(1)}, f32[1024]{0:T(1024)S(1)}, u32[]{:S(2)}, u32[]{:S(2)}) collective-permute-start(f32[1024]{0:T(1024)S(1)} %bitcast.185), channel_id=1, source_target_pairs={{4,0},{8,4},{12,8},{16,12},{20,16},{24,20},{28,24},{0,28},{5,1},{9... | collective-permute-start | bytes 12296 | tf_op jit(solution)/shard_map/ppermute | solution.py:29
  22.1 3.2 %fusion.109 = (f32[255,1024]{1,0:T(8,128)}, f32[255,1024]{1,0:T(8,128)}) fusion(f32[256,1024]{1,0:T(8,128)} %param.18), kind=kLoop, calls=%fused_computation.273 | loop fusion | bytes 4177920 | tf_op jit(solution)/shard_map/slice | solution.py:36
  25.3 1.7 fusion.108
  28.6 4.5 %gather_fusion.1 = f32[1024]{0:T(1024)S(1)} fusion(f32[1024]{0:T(1024)S(1)} %broadcast_select_fusion.7, s32[1024]{0:T(1024)S(1)} %fusion.82), kind=kCustom, calls=%fused_computation.clone | custom fusion | bytes 12288 | tf_op jit(solution)/shard_map/jit(_take)/gather | solution.py:122
  33.2 5.1 %fusion.22 = (f32[256,1024]{1,0:T(8,128)S(1)}, f32[256,1024]{1,0:T(8,128)S(1)}) fusion(f32[256,1024]{1,0:T(8,128)S(1)} %copy-done, f32[255,1024]{1,0:T(8,128)} %get-tuple-element.332, f32[1,1024]{1,0:T(1,128)S(1)} %bitcast.169, f32[1,1024]{1,0:T(1,128)S(1)} %bitcast.172, f32[255,1024]{1,0:T(8,128)} %get-tuple-element.331, ...), kind=kLoop, calls=%fused_computation.51 | loop fusion | flops 4718592 | bytes 12582912 | tf_op jit(solution)/shard_map/add | solution.py:41
  39.9 4.0 %collective-permute-start.6 = (f32[1,256]{1,0:T(1,128)S(1)}, f32[1,256]{1,0:T(1,128)S(1)}, u32[]{:S(2)}, u32[]{:S(2)}) collective-permute-start(f32[1,256]{1,0:T(1,128)S(1)} %bitcast.206), channel_id=1, source_target_pairs={{0,1},{1,2},{2,3},{4,5},{5,6},{6,7},{8,9},{9,10},{10,11},{12,13},{... | collective-permute-start | bytes 3080 | tf_op jit(solution)/shard_map/ppermute | solution.py:20
  45.4 4.7 %collective-permute-start.5 = (f32[1024]{0:T(1024)S(1)}, f32[1024]{0:T(1024)S(1)}, u32[]{:S(2)}, u32[]{:S(2)}) collective-permute-start(f32[1024]{0:T(1024)S(1)} %bitcast.189), channel_id=1, source_target_pairs={{4,0},{8,4},{12,8},{16,12},{20,16},{24,20},{28,24},{0,28},{5,1},{9... | collective-permute-start | bytes 12296 | tf_op jit(solution)/shard_map/ppermute | solution.py:29
  52.2 4.5 %gather_fusion.2 = f32[1024]{0:T(1024)S(1)} fusion(f32[1024]{0:T(1024)S(1)} %broadcast_select_fusion.6, s32[1024]{0:T(1024)S(1)} %fusion.82), kind=kCustom, calls=%fused_computation.2.clone | custom fusion | bytes 12288 | tf_op jit(solution)/shard_map/jit(_take)/gather | solution.py:122
  56.7 4.8 %fusion.27 = f32[256,1024]{1,0:T(8,128)S(1)} fusion(f32[256,1024]{1,0:T(8,128)S(1)} %copy-done, f32[255,1024]{1,0:T(8,128)} %get-tuple-element.326, f32[1,1024]{1,0:T(1,128)S(1)} %bitcast.174, f32[1,1024]{1,0:T(1,128)S(1)} %bitcast.173, f32[255,1024]{1,0:T(8,128)} %get-tuple-element.325, f32[256,1023]{1,0:T(8,128)} %get-tuple-element.324, ...), kind=kLoop, calls=%fused_computation.60 | loop fusion | flops 3670016 | bytes 12582912 | tf_op jit(solution)/shard_map/add | solution.py:41
  63.2 4.1 %collective-permute-start.10 = (f32[1,256]{1,0:T(1,128)S(1)}, f32[1,256]{1,0:T(1,128)S(1)}, u32[]{:S(2)}, u32[]{:S(2)}) collective-permute-start(f32[1,256]{1,0:T(1,128)S(1)} %bitcast.216), channel_id=1, source_target_pairs={{0,1},{1,2},{2,3},{4,5},{5,6},{6,7},{8,9},{9,10},{10,11},{12,13},{... | collective-permute-start | bytes 3080 | tf_op jit(solution)/shard_map/ppermute | solution.py:20
  68.8 4.8 %collective-permute-start.9 = (f32[1024]{0:T(1024)S(1)}, f32[1024]{0:T(1024)S(1)}, u32[]{:S(2)}, u32[]{:S(2)}) collective-permute-start(f32[1024]{0:T(1024)S(1)} %bitcast.198), channel_id=1, source_target_pairs={{4,0},{8,4},{12,8},{16,12},{20,16},{24,20},{28,24},{0,28},{5,1},{9... | collective-permute-start | bytes 12296 | tf_op jit(solution)/shard_map/ppermute | solution.py:29
  75.5 4.5 %gather_fusion.3 = f32[1024]{0:T(1024)S(1)} fusion(f32[1024]{0:T(1024)S(1)} %broadcast_select_fusion.5, s32[1024]{0:T(1024)S(1)} %fusion.82), kind=kCustom, calls=%fused_computation.3.clone | custom fusion | bytes 12288 | tf_op jit(solution)/shard_map/jit(_take)/gather | solution.py:122
  80.1 5.1 %fusion.32 = f32[256,1024]{1,0:T(8,128)S(1)} fusion(f32[256,1024]{1,0:T(8,128)S(1)} %copy-done, f32[255,1024]{1,0:T(8,128)} %get-tuple-element.320, f32[1,1024]{1,0:T(1,128)S(1)} %bitcast.176, f32[1,1024]{1,0:T(1,128)S(1)} %bitcast.175, f32[255,1024]{1,0:T(8,128)} %get-tuple-element.319, f32[256,1023]{1,0:T(8,128)} %get-tuple-element.318, ...), kind=kLoop, calls=%fused_computation.69 | loop fusion | flops 3670016 | bytes 12582912 | tf_op jit(solution)/shard_map/add | solution.py:41
  86.9 4.3 %collective-permute-start.14 = (f32[1,256]{1,0:T(1,128)S(1)}, f32[1,256]{1,0:T(1,128)S(1)}, u32[]{:S(2)}, u32[]{:S(2)}) collective-permute-start(f32[1,256]{1,0:T(1,128)S(1)} %bitcast.205), channel_id=1, source_target_pairs={{0,1},{1,2},{2,3},{4,5},{5,6},{6,7},{8,9},{9,10},{10,11},{12,13},{... | collective-permute-start | bytes 3080 | tf_op jit(solution)/shard_map/ppermute | solution.py:20
  92.6 4.7 %collective-permute-start.13 = (f32[1024]{0:T(1024)S(1)}, f32[1024]{0:T(1024)S(1)}, u32[]{:S(2)}, u32[]{:S(2)}) collective-permute-start(f32[1024]{0:T(1024)S(1)} %bitcast.190), channel_id=1, source_target_pairs={{4,0},{8,4},{12,8},{16,12},{20,16},{24,20},{28,24},{0,28},{5,1},{9... | collective-permute-start | bytes 12296 | tf_op jit(solution)/shard_map/ppermute | solution.py:29
  99.3 4.5 %gather_fusion.4 = f32[1024]{0:T(1024)S(1)} fusion(f32[1024]{0:T(1024)S(1)} %broadcast_select_fusion.4, s32[1024]{0:T(1024)S(1)} %fusion.82), kind=kCustom, calls=%fused_computation.4.clone | custom fusion | bytes 12288 | tf_op jit(solution)/shard_map/jit(_take)/gather | solution.py:122
  103.8 4.8 %fusion.37 = f32[256,1024]{1,0:T(8,128)S(1)} fusion(f32[256,1024]{1,0:T(8,128)S(1)} %copy-done, f32[255,1024]{1,0:T(8,128)} %get-tuple-element.314, f32[1,1024]{1,0:T(1,128)S(1)} %bitcast.178, f32[1,1024]{1,0:T(1,128)S(1)} %bitcast.177, f32[255,1024]{1,0:T(8,128)} %get-tuple-element.313, f32[256,1023]{1,0:T(8,128)} %get-tuple-element.312, ...), kind=kLoop, calls=%fused_computation.78 | loop fusion | flops 3670016 | bytes 12582912 | tf_op jit(solution)/shard_map/add | solution.py:41
  110.4 4.4 %collective-permute-start.18 = (f32[1,256]{1,0:T(1,128)S(1)}, f32[1,256]{1,0:T(1,128)S(1)}, u32[]{:S(2)}, u32[]{:S(2)}) collective-permute-start(f32[1,256]{1,0:T(1,128)S(1)} %bitcast.217), channel_id=1, source_target_pairs={{0,1},{1,2},{2,3},{4,5},{5,6},{6,7},{8,9},{9,10},{10,11},{12,13},{... | collective-permute-start | bytes 3080 | tf_op jit(solution)/shard_map/ppermute | solution.py:20
  116.2 4.8 %collective-permute-start.17 = (f32[1024]{0:T(1024)S(1)}, f32[1024]{0:T(1024)S(1)}, u32[]{:S(2)}, u32[]{:S(2)}) collective-permute-start(f32[1024]{0:T(1024)S(1)} %bitcast.199), channel_id=1, source_target_pairs={{4,0},{8,4},{12,8},{16,12},{20,16},{24,20},{28,24},{0,28},{5,1},{9... | collective-permute-start | bytes 12296 | tf_op jit(solution)/shard_map/ppermute | solution.py:29
  122.9 4.5 %gather_fusion.5 = f32[1024]{0:T(1024)S(1)} fusion(f32[1024]{0:T(1024)S(1)} %broadcast_select_fusion.3, s32[1024]{0:T(1024)S(1)} %fusion.82), kind=kCustom, calls=%fused_computation.5.clone | custom fusion | bytes 12288 | tf_op jit(solution)/shard_map/jit(_take)/gather | solution.py:122
  127.5 5.1 %fusion.42 = f32[256,1024]{1,0:T(8,128)S(1)} fusion(f32[256,1024]{1,0:T(8,128)S(1)} %copy-done, f32[255,1024]{1,0:T(8,128)} %get-tuple-element.308, f32[1,1024]{1,0:T(1,128)S(1)} %bitcast.180, f32[1,1024]{1,0:T(1,128)S(1)} %bitcast.179, f32[255,1024]{1,0:T(8,128)} %get-tuple-element.307, f32[256,1023]{1,0:T(8,128)} %get-tuple-element.306, ...), kind=kLoop, calls=%fused_computation.87 | loop fusion | flops 3670016 | bytes 12582912 | tf_op jit(solution)/shard_map/add | solution.py:41
  134.2 4.1 %collective-permute-start.22 = (f32[1,256]{1,0:T(1,128)S(1)}, f32[1,256]{1,0:T(1,128)S(1)}, u32[]{:S(2)}, u32[]{:S(2)}) collective-permute-start(f32[1,256]{1,0:T(1,128)S(1)} %bitcast.207), channel_id=1, source_target_pairs={{0,1},{1,2},{2,3},{4,5},{5,6},{6,7},{8,9},{9,10},{10,11},{12,13},{... | collective-permute-start | bytes 3080 | tf_op jit(solution)/shard_map/ppermute | solution.py:20
  139.7 3.5 %collective-permute-start.21 = (f32[1024]{0:T(1024)S(1)}, f32[1024]{0:T(1024)S(1)}, u32[]{:S(2)}, u32[]{:S(2)}) collective-permute-start(f32[1024]{0:T(1024)S(1)} %bitcast.191), channel_id=1, source_target_pairs={{4,0},{8,4},{12,8},{16,12},{20,16},{24,20},{28,24},{0,28},{5,1},{9... | collective-permute-start | bytes 12296 | tf_op jit(solution)/shard_map/ppermute | solution.py:29
  143.3 1.6 fusion.93
  145.3 4.3 %collective-permute-done.20 = f32[1024]{0:T(1024)S(1)} collective-permute-done((f32[1024]{0:T(1024)S(1)}, f32[1024]{0:T(1024)S(1)}, u32[]{:S(2)}, u32[]{:S(2)}) %collective-permute-start.20) | collective-permute-done | bytes 4128 | tf_op jit(solution)/shard_map/ppermute | solution.py:29
  149.6 4.5 %gather_fusion.6 = f32[1024]{0:T(1024)S(1)} fusion(f32[1024]{0:T(1024)S(1)} %broadcast_select_fusion.2, s32[1024]{0:T(1024)S(1)} %fusion.82), kind=kCustom, calls=%fused_computation.6.clone | custom fusion | bytes 12288 | tf_op jit(solution)/shard_map/jit(_take)/gather | solution.py:122
  154.2 4.8 %fusion.47 = f32[256,1024]{1,0:T(8,128)S(1)} fusion(f32[256,1024]{1,0:T(8,128)S(1)} %copy-done, f32[255,1024]{1,0:T(8,128)} %get-tuple-element.302, f32[1,1024]{1,0:T(1,128)S(1)} %bitcast.182, f32[1,1024]{1,0:T(1,128)S(1)} %bitcast.181, f32[255,1024]{1,0:T(8,128)} %get-tuple-element.301, f32[256,1023]{1,0:T(8,128)} %get-tuple-element.300, ...), kind=kLoop, calls=%fused_computation.96 | loop fusion | flops 3670016 | bytes 12582912 | tf_op jit(solution)/shard_map/add | solution.py:41
  160.7 4.3 %collective-permute-start.26 = (f32[1,256]{1,0:T(1,128)S(1)}, f32[1,256]{1,0:T(1,128)S(1)}, u32[]{:S(2)}, u32[]{:S(2)}) collective-permute-start(f32[1,256]{1,0:T(1,128)S(1)} %bitcast.218), channel_id=1, source_target_pairs={{0,1},{1,2},{2,3},{4,5},{5,6},{6,7},{8,9},{9,10},{10,11},{12,13},{... | collective-permute-start | bytes 3080 | tf_op jit(solution)/shard_map/ppermute | solution.py:20
  166.4 4.8 %collective-permute-start.25 = (f32[1024]{0:T(1024)S(1)}, f32[1024]{0:T(1024)S(1)}, u32[]{:S(2)}, u32[]{:S(2)}) collective-permute-start(f32[1024]{0:T(1024)S(1)} %bitcast.200), channel_id=1, source_target_pairs={{4,0},{8,4},{12,8},{16,12},{20,16},{24,20},{28,24},{0,28},{5,1},{9... | collective-permute-start | bytes 12296 | tf_op jit(solution)/shard_map/ppermute | solution.py:29
  173.1 4.5 %gather_fusion.7 = f32[1024]{0:T(1024)S(1)} fusion(f32[1024]{0:T(1024)S(1)} %broadcast_select_fusion.1, s32[1024]{0:T(1024)S(1)} %fusion.82), kind=kCustom, calls=%fused_computation.7.clone | custom fusion | bytes 12288 | tf_op jit(solution)/shard_map/jit(_take)/gather | solution.py:122
  177.7 5.1 %fusion.52 = f32[256,1024]{1,0:T(8,128)S(1)} fusion(f32[256,1024]{1,0:T(8,128)S(1)} %copy-done, f32[255,1024]{1,0:T(8,128)} %get-tuple-element.296, f32[1,1024]{1,0:T(1,128)S(1)} %bitcast.184, f32[1,1024]{1,0:T(1,128)S(1)} %bitcast.183, f32[255,1024]{1,0:T(8,128)} %get-tuple-element.295, f32[256,1023]{1,0:T(8,128)} %get-tuple-element.294, ...), kind=kLoop, calls=%fused_computation.105 | loop fusion | flops 3670016 | bytes 12582912 | tf_op jit(solution)/shard_map/add | solution.py:41
  184.6 5.1 %collective-permute-start.30 = (f32[1,256]{1,0:T(1,128)S(1)}, f32[1,256]{1,0:T(1,128)S(1)}, u32[]{:S(2)}, u32[]{:S(2)}) collective-permute-start(f32[1,256]{1,0:T(1,128)S(1)} %bitcast.210), channel_id=1, source_target_pairs={{0,1},{1,2},{2,3},{4,5},{5,6},{6,7},{8,9},{9,10},{10,11},{12,13},{... | collective-permute-start | bytes 3080 | tf_op jit(solution)/shard_map/ppermute | solution.py:20
  191.1 4.7 %collective-permute-start.29 = (f32[1024]{0:T(1024)S(1)}, f32[1024]{0:T(1024)S(1)}, u32[]{:S(2)}, u32[]{:S(2)}) collective-permute-start(f32[1024]{0:T(1024)S(1)} %bitcast.188), channel_id=1, source_target_pairs={{4,0},{8,4},{12,8},{16,12},{20,16},{24,20},{28,24},{0,28},{5,1},{9... | collective-permute-start | bytes 12296 | tf_op jit(solution)/shard_map/ppermute | solution.py:29
  197.8 4.5 %gather_fusion.8 = f32[1024]{0:T(1024)S(1)} fusion(f32[1024]{0:T(1024)S(1)} %broadcast_select_fusion, s32[1024]{0:T(1024)S(1)} %fusion.82), kind=kCustom, calls=%fused_computation.8.clone | custom fusion | bytes 12288 | tf_op jit(solution)/shard_map/jit(_take)/gather | solution.py:122
  202.3 4.8 %fusion.57 = f32[256,1024]{1,0:T(8,128)S(1)} fusion(f32[256,1024]{1,0:T(8,128)S(1)} %copy-done, f32[255,1024]{1,0:T(8,128)} %get-tuple-element.290, f32[1,1024]{1,0:T(1,128)S(1)} %bitcast.171, f32[1,1024]{1,0:T(1,128)S(1)} %bitcast.170, f32[255,1024]{1,0:T(8,128)} %get-tuple-element.289, f32[256,1023]{1,0:T(8,128)} %get-tuple-element.288, ...), kind=kLoop, calls=%fused_computation.114 | loop fusion | flops 3670016 | bytes 12582912 | tf_op jit(solution)/shard_map/add | solution.py:41
  209.4 22.8 %while.13 = (s32[]{:T(128)}, f32[4,256,128]{2,1,0:T(8,128)}, f32[1024]{0:T(1024)S(1)}, f32[1,1024]{1,0:T(1,128)S(1)}, f32[]{:T(128)}, /*index=5*/f32[1024]{0:T(1...) while((s32[]{:T(128)}, f32[4,256,128]{2,1,0:T(8,128)}, ...), condition=%wide.region_1.3_spmd, body=%wide.region_0.2_spmd.sunk | while | flops 141568512 | bytes 2851517 | solution.py:150
  210.8 1.8 gather_fusion
  216.5 1.8 gather_fusion
  222.2 1.8 gather_fusion
  227.9 1.8 gather_fusion
  232.3 25.9 %reduce-scatter.2.cloned.1.call-done = f32[256,128]{1,0:T(8,128)} async-done(((f32[1024,128]{1,0:T(8,128)}), f32[256,128]{1,0:T(8,128)}) %reduce-scatter.2.cloned.1.call-update) | async-done | bytes 131088 | tf_op jit(solution)/shard_map/reduce_scatter | solution.py:153
  259.6 3.8 %collective-permute-done.32 = f32[256,128]{1,0:T(8,128)S(1)} collective-permute-done((f32[256,128]{1,0:T(8,128)}, f32[256,128]{1,0:T(8,128)S(1)}, u32[]{:S(2)}, u32[]{:S(2)}) %collective-permute-start.32) | collective-permute-done | bytes 131104 | tf_op jit(solution)/shard_map/ppermute | solution.py:162
  266.1 3.3 %collective-permute-done.33 = f32[256,128]{1,0:T(8,128)S(1)} collective-permute-done((f32[256,128]{1,0:T(8,128)S(1)}, f32[256,128]{1,0:T(8,128)S(1)}, u32[]{:S(2)}, u32[]{:S(2)}) %collective-permute-start.33) | collective-permute-done | bytes 131104 | tf_op jit(solution)/shard_map/ppermute | solution.py:162
  269.4 2.5 collective-permute-start.34
  271.9 4.9 %collective-permute-done.34 = f32[256,128]{1,0:T(8,128)S(1)} collective-permute-done((f32[256,128]{1,0:T(8,128)S(1)}, f32[256,128]{1,0:T(8,128)S(1)}, u32[]{:S(2)}, u32[]{:S(2)}) %collective-permute-start.34) | collective-permute-done | bytes 131104 | tf_op jit(solution)/shard_map/ppermute | solution.py:162
  276.9 6.1 %psum.7 = f32[16,128]{1,0:T(8,128)S(1)} all-reduce(f32[16,128]{1,0:T(8,128)S(1)} %fusion.66), channel_id=1, replica_groups=mesh['pass'=8,'cell'=4] {'cell'}, use_global_device_ids=true, to_apply=%region_3.5 | all-reduce | flops 2048 | bytes 16384 | tf_op jit(solution)/shard_map/psum | solution.py:174
  (235 shorter events, 61.1 us)
Async XLA Ops:
  7.2 18.1 %copy-start.4 = (f32[256,1024]{1,0:T(8,128)S(1)}, f32[256,1024]{1,0:T(8,128)}, u32[]{:S(2)}) copy-start(f32[256,1024]{1,0:T(8,128)} %param.18) | copy-start | bytes 3145732
  7.2 251.0 %reduce-scatter.2.cloned.1.call-start = ((), (), s32[]{:S(2)}) async-start(), calls=%async_computation.1 | async-start | bytes 655360 | tf_op jit(solution)/shard_map/reduce_scatter | solution.py:153
  8.5 19.9 %collective-permute-start.2 = (f32[1,256]{1,0:T(1,128)S(1)}, f32[1,256]{1,0:T(1,128)S(1)}, u32[]{:S(2)}, u32[]{:S(2)}) collective-permute-start(f32[1,256]{1,0:T(1,128)S(1)} %bitcast.202), channel_id=1, source_target_pairs={{0,1},{1,2},{2,3},{4,5},{5,6},{6,7},{8,9},{9,10},{10,11},{12,13},{... | collective-permute-start | bytes 3080 | tf_op jit(solution)/shard_map/ppermute | solution.py:20
  10.9 17.4 %collective-permute-start.3 = (f32[1,256]{1,0:T(1,128)S(1)}, f32[1,256]{1,0:T(1,128)S(1)}, u32[]{:S(2)}, u32[]{:S(2)}) collective-permute-start(f32[1,256]{1,0:T(1,128)S(1)} %bitcast.203), channel_id=1, source_target_pairs={{1,0},{2,1},{3,2},{5,4},{6,5},{7,6},{9,8},{10,9},{11,10},{13,12},{... | collective-permute-start | bytes 3080 | tf_op jit(solution)/shard_map/ppermute | solution.py:21
  16.5 12.0 %collective-permute-start = (f32[1024]{0:T(1024)S(1)}, f32[1024]{0:T(1024)S(1)}, u32[]{:S(2)}, u32[]{:S(2)}) collective-permute-start(f32[1024]{0:T(1024)S(1)} %bitcast.186), channel_id=1, source_target_pairs={{28,0},{0,4},{4,8},{8,12},{12,16},{16,20},{20,24},{24,28},{29,1},{... | collective-permute-start | bytes 12296 | tf_op jit(solution)/shard_map/ppermute | solution.py:29
  18.9 9.7 %collective-permute-start.1 = (f32[1024]{0:T(1024)S(1)}, f32[1024]{0:T(1024)S(1)}, u32[]{:S(2)}, u32[]{:S(2)}) collective-permute-start(f32[1024]{0:T(1024)S(1)} %bitcast.185), channel_id=1, source_target_pairs={{4,0},{8,4},{12,8},{16,12},{20,16},{24,20},{28,24},{0,28},{5,1},{9... | collective-permute-start | bytes 12296 | tf_op jit(solution)/shard_map/ppermute | solution.py:29
  22.0 5.1 %copy-start.13 = (f32[2,1024]{1,0:T(2,128)S(1)}, f32[2,1024]{1,0:T(2,128)}, u32[]{:S(2)}) copy-start(f32[2,1024]{1,0:T(2,128)} %param.25) | copy-start | bytes 24580
  22.0 5.1 %copy-start.14 = (f32[2,1024]{1,0:T(2,128)S(1)}, f32[2,1024]{1,0:T(2,128)}, u32[]{:S(2)}) copy-start(f32[2,1024]{1,0:T(2,128)} %param.26) | copy-start | bytes 24580
  22.0 5.1 %copy-start.15 = (f32[2,1024]{1,0:T(2,128)S(1)}, f32[2,1024]{1,0:T(2,128)}, u32[]{:S(2)}) copy-start(f32[2,1024]{1,0:T(2,128)} %param.29) | copy-start | bytes 24580
  22.0 5.2 %copy-start.8 = (f32[3,1024]{1,0:T(4,128)S(1)}, f32[3,1024]{1,0:T(4,128)}, u32[]{:S(2)}) copy-start(f32[3,1024]{1,0:T(4,128)} %param.30) | copy-start | bytes 36868
  25.3 7.9 %copy-start = (f32[256,1024]{1,0:T(8,128)S(1)}, f32[256,1024]{1,0:T(8,128)}, u32[]{:S(2)}) copy-start(f32[256,1024]{1,0:T(8,128)} %param.20) | copy-start | bytes 3145732
  38.2 7.1 %copy-start.7 = (f32[1,8,1024]{2,1,0:T(8,128)S(1)}, f32[1,8,1024]{2,1,0:T(8,128)}, u32[]{:S(2)}) copy-start(f32[1,8,1024]{2,1,0:T(8,128)} %param.21) | copy-start | bytes 98308
  39.9 12.0 %collective-permute-start.6 = (f32[1,256]{1,0:T(1,128)S(1)}, f32[1,256]{1,0:T(1,128)S(1)}, u32[]{:S(2)}, u32[]{:S(2)}) collective-permute-start(f32[1,256]{1,0:T(1,128)S(1)} %bitcast.206), channel_id=1, source_target_pairs={{0,1},{1,2},{2,3},{4,5},{5,6},{6,7},{8,9},{9,10},{10,11},{12,13},{... | collective-permute-start | bytes 3080 | tf_op jit(solution)/shard_map/ppermute | solution.py:20
  44.0 7.8 %collective-permute-start.7 = (f32[1,256]{1,0:T(1,128)S(1)}, f32[1,256]{1,0:T(1,128)S(1)}, u32[]{:S(2)}, u32[]{:S(2)}) collective-permute-start(f32[1,256]{1,0:T(1,128)S(1)} %bitcast.211), channel_id=1, source_target_pairs={{1,0},{2,1},{3,2},{5,4},{6,5},{7,6},{9,8},{10,9},{11,10},{13,12},{... | collective-permute-start | bytes 3080 | tf_op jit(solution)/shard_map/ppermute | solution.py:21
  45.4 6.8 %collective-permute-start.4 = (f32[1024]{0:T(1024)S(1)}, f32[1024]{0:T(1024)S(1)}, u32[]{:S(2)}, u32[]{:S(2)}) collective-permute-start(f32[1024]{0:T(1024)S(1)} %bitcast.192), channel_id=1, source_target_pairs={{28,0},{0,4},{4,8},{8,12},{12,16},{16,20},{20,24},{24,28},{29,1},{... | collective-permute-start | bytes 12296 | tf_op jit(solution)/shard_map/ppermute | solution.py:29
  45.4 6.7 %collective-permute-start.5 = (f32[1024]{0:T(1024)S(1)}, f32[1024]{0:T(1024)S(1)}, u32[]{:S(2)}, u32[]{:S(2)}) collective-permute-start(f32[1024]{0:T(1024)S(1)} %bitcast.189), channel_id=1, source_target_pairs={{4,0},{8,4},{12,8},{16,12},{20,16},{24,20},{28,24},{0,28},{5,1},{9... | collective-permute-start | bytes 12296 | tf_op jit(solution)/shard_map/ppermute | solution.py:29
  61.5 13.7 %copy-start.1 = (f32[256,1024]{1,0:T(8,128)}, f32[256,1024]{1,0:T(8,128)S(1)}, u32[]{:S(2)}) copy-start(f32[256,1024]{1,0:T(8,128)S(1)} %fusion.27) | copy-start | bytes 3145732
  63.2 12.1 %collective-permute-start.10 = (f32[1,256]{1,0:T(1,128)S(1)}, f32[1,256]{1,0:T(1,128)S(1)}, u32[]{:S(2)}, u32[]{:S(2)}) collective-permute-start(f32[1,256]{1,0:T(1,128)S(1)} %bitcast.216), channel_id=1, source_target_pairs={{0,1},{1,2},{2,3},{4,5},{5,6},{6,7},{8,9},{9,10},{10,11},{12,13},{... | collective-permute-start | bytes 3080 | tf_op jit(solution)/shard_map/ppermute | solution.py:20
  67.3 7.8 %collective-permute-start.11 = (f32[1,256]{1,0:T(1,128)S(1)}, f32[1,256]{1,0:T(1,128)S(1)}, u32[]{:S(2)}, u32[]{:S(2)}) collective-permute-start(f32[1,256]{1,0:T(1,128)S(1)} %bitcast.222), channel_id=1, source_target_pairs={{1,0},{2,1},{3,2},{5,4},{6,5},{7,6},{9,8},{10,9},{11,10},{13,12},{... | collective-permute-start | bytes 3080 | tf_op jit(solution)/shard_map/ppermute | solution.py:21
  68.7 6.8 %collective-permute-start.8 = (f32[1024]{0:T(1024)S(1)}, f32[1024]{0:T(1024)S(1)}, u32[]{:S(2)}, u32[]{:S(2)}) collective-permute-start(f32[1024]{0:T(1024)S(1)} %bitcast.195), channel_id=1, source_target_pairs={{28,0},{0,4},{4,8},{8,12},{12,16},{16,20},{20,24},{24,28},{29,1},{... | collective-permute-start | bytes 12296 | tf_op jit(solution)/shard_map/ppermute | solution.py:29
  68.8 6.7 %collective-permute-start.9 = (f32[1024]{0:T(1024)S(1)}, f32[1024]{0:T(1024)S(1)}, u32[]{:S(2)}, u32[]{:S(2)}) collective-permute-start(f32[1024]{0:T(1024)S(1)} %bitcast.198), channel_id=1, source_target_pairs={{4,0},{8,4},{12,8},{16,12},{20,16},{24,20},{28,24},{0,28},{5,1},{9... | collective-permute-start | bytes 12296 | tf_op jit(solution)/shard_map/ppermute | solution.py:29
  86.9 12.3 %collective-permute-start.14 = (f32[1,256]{1,0:T(1,128)S(1)}, f32[1,256]{1,0:T(1,128)S(1)}, u32[]{:S(2)}, u32[]{:S(2)}) collective-permute-start(f32[1,256]{1,0:T(1,128)S(1)} %bitcast.205), channel_id=1, source_target_pairs={{0,1},{1,2},{2,3},{4,5},{5,6},{6,7},{8,9},{9,10},{10,11},{12,13},{... | collective-permute-start | bytes 3080 | tf_op jit(solution)/shard_map/ppermute | solution.py:20
  91.1 7.8 %collective-permute-start.15 = (f32[1,256]{1,0:T(1,128)S(1)}, f32[1,256]{1,0:T(1,128)S(1)}, u32[]{:S(2)}, u32[]{:S(2)}) collective-permute-start(f32[1,256]{1,0:T(1,128)S(1)} %bitcast.208), channel_id=1, source_target_pairs={{1,0},{2,1},{3,2},{5,4},{6,5},{7,6},{9,8},{10,9},{11,10},{13,12},{... | collective-permute-start | bytes 3080 | tf_op jit(solution)/shard_map/ppermute | solution.py:21
  92.5 6.8 %collective-permute-start.12 = (f32[1024]{0:T(1024)S(1)}, f32[1024]{0:T(1024)S(1)}, u32[]{:S(2)}, u32[]{:S(2)}) collective-permute-start(f32[1024]{0:T(1024)S(1)} %bitcast.193), channel_id=1, source_target_pairs={{28,0},{0,4},{4,8},{8,12},{12,16},{16,20},{20,24},{24,28},{29,1},{... | collective-permute-start | bytes 12296 | tf_op jit(solution)/shard_map/ppermute | solution.py:29
  92.6 6.7 %collective-permute-start.13 = (f32[1024]{0:T(1024)S(1)}, f32[1024]{0:T(1024)S(1)}, u32[]{:S(2)}, u32[]{:S(2)}) collective-permute-start(f32[1024]{0:T(1024)S(1)} %bitcast.190), channel_id=1, source_target_pairs={{4,0},{8,4},{12,8},{16,12},{20,16},{24,20},{28,24},{0,28},{5,1},{9... | collective-permute-start | bytes 12296 | tf_op jit(solution)/shard_map/ppermute | solution.py:29
  108.6 13.9 %copy-start.2 = (f32[256,1024]{1,0:T(8,128)}, f32[256,1024]{1,0:T(8,128)S(1)}, u32[]{:S(2)}) copy-start(f32[256,1024]{1,0:T(8,128)S(1)} %fusion.37) | copy-start | bytes 3145732
  110.4 12.4 %collective-permute-start.18 = (f32[1,256]{1,0:T(1,128)S(1)}, f32[1,256]{1,0:T(1,128)S(1)}, u32[]{:S(2)}, u32[]{:S(2)}) collective-permute-start(f32[1,256]{1,0:T(1,128)S(1)} %bitcast.217), channel_id=1, source_target_pairs={{0,1},{1,2},{2,3},{4,5},{5,6},{6,7},{8,9},{9,10},{10,11},{12,13},{... | collective-permute-start | bytes 3080 | tf_op jit(solution)/shard_map/ppermute | solution.py:20
  114.7 7.8 %collective-permute-start.19 = (f32[1,256]{1,0:T(1,128)S(1)}, f32[1,256]{1,0:T(1,128)S(1)}, u32[]{:S(2)}, u32[]{:S(2)}) collective-permute-start(f32[1,256]{1,0:T(1,128)S(1)} %bitcast.224), channel_id=1, source_target_pairs={{1,0},{2,1},{3,2},{5,4},{6,5},{7,6},{9,8},{10,9},{11,10},{13,12},{... | collective-permute-start | bytes 3080 | tf_op jit(solution)/shard_map/ppermute | solution.py:21
  116.1 6.8 %collective-permute-start.16 = (f32[1024]{0:T(1024)S(1)}, f32[1024]{0:T(1024)S(1)}, u32[]{:S(2)}, u32[]{:S(2)}) collective-permute-start(f32[1024]{0:T(1024)S(1)} %bitcast.196), channel_id=1, source_target_pairs={{28,0},{0,4},{4,8},{8,12},{12,16},{16,20},{20,24},{24,28},{29,1},{... | collective-permute-start | bytes 12296 | tf_op jit(solution)/shard_map/ppermute | solution.py:29
  116.2 6.7 %collective-permute-start.17 = (f32[1024]{0:T(1024)S(1)}, f32[1024]{0:T(1024)S(1)}, u32[]{:S(2)}, u32[]{:S(2)}) collective-permute-start(f32[1024]{0:T(1024)S(1)} %bitcast.199), channel_id=1, source_target_pairs={{4,0},{8,4},{12,8},{16,12},{20,16},{24,20},{28,24},{0,28},{5,1},{9... | collective-permute-start | bytes 12296 | tf_op jit(solution)/shard_map/ppermute | solution.py:29
  134.2 10.9 %collective-permute-start.22 = (f32[1,256]{1,0:T(1,128)S(1)}, f32[1,256]{1,0:T(1,128)S(1)}, u32[]{:S(2)}, u32[]{:S(2)}) collective-permute-start(f32[1,256]{1,0:T(1,128)S(1)} %bitcast.207), channel_id=1, source_target_pairs={{0,1},{1,2},{2,3},{4,5},{5,6},{6,7},{8,9},{9,10},{10,11},{12,13},{... | collective-permute-start | bytes 3080 | tf_op jit(solution)/shard_map/ppermute | solution.py:20
  138.4 6.6 %collective-permute-start.23 = (f32[1,256]{1,0:T(1,128)S(1)}, f32[1,256]{1,0:T(1,128)S(1)}, u32[]{:S(2)}, u32[]{:S(2)}) collective-permute-start(f32[1,256]{1,0:T(1,128)S(1)} %bitcast.213), channel_id=1, source_target_pairs={{1,0},{2,1},{3,2},{5,4},{6,5},{7,6},{9,8},{10,9},{11,10},{13,12},{... | collective-permute-start | bytes 3080 | tf_op jit(solution)/shard_map/ppermute | solution.py:21
  139.7 5.6 %collective-permute-start.21 = (f32[1024]{0:T(1024)S(1)}, f32[1024]{0:T(1024)S(1)}, u32[]{:S(2)}, u32[]{:S(2)}) collective-permute-start(f32[1024]{0:T(1024)S(1)} %bitcast.191), channel_id=1, source_target_pairs={{4,0},{8,4},{12,8},{16,12},{20,16},{24,20},{28,24},{0,28},{5,1},{9... | collective-permute-start | bytes 12296 | tf_op jit(solution)/shard_map/ppermute | solution.py:29
  143.3 6.4 %collective-permute-start.20 = (f32[1024]{0:T(1024)S(1)}, f32[1024]{0:T(1024)S(1)}, u32[]{:S(2)}, u32[]{:S(2)}) collective-permute-start(f32[1024]{0:T(1024)S(1)} %bitcast.194), channel_id=1, source_target_pairs={{28,0},{0,4},{4,8},{8,12},{12,16},{16,20},{20,24},{24,28},{29,1},{... | collective-permute-start | bytes 12296 | tf_op jit(solution)/shard_map/ppermute | solution.py:29
  159.0 13.8 %copy-start.3 = (f32[256,1024]{1,0:T(8,128)}, f32[256,1024]{1,0:T(8,128)S(1)}, u32[]{:S(2)}) copy-start(f32[256,1024]{1,0:T(8,128)S(1)} %fusion.47) | copy-start | bytes 3145732
  160.7 12.3 %collective-permute-start.26 = (f32[1,256]{1,0:T(1,128)S(1)}, f32[1,256]{1,0:T(1,128)S(1)}, u32[]{:S(2)}, u32[]{:S(2)}) collective-permute-start(f32[1,256]{1,0:T(1,128)S(1)} %bitcast.218), channel_id=1, source_target_pairs={{0,1},{1,2},{2,3},{4,5},{5,6},{6,7},{8,9},{9,10},{10,11},{12,13},{... | collective-permute-start | bytes 3080 | tf_op jit(solution)/shard_map/ppermute | solution.py:20
  165.0 7.8 %collective-permute-start.27 = (f32[1,256]{1,0:T(1,128)S(1)}, f32[1,256]{1,0:T(1,128)S(1)}, u32[]{:S(2)}, u32[]{:S(2)}) collective-permute-start(f32[1,256]{1,0:T(1,128)S(1)} %bitcast.226), channel_id=1, source_target_pairs={{1,0},{2,1},{3,2},{5,4},{6,5},{7,6},{9,8},{10,9},{11,10},{13,12},{... | collective-permute-start | bytes 3080 | tf_op jit(solution)/shard_map/ppermute | solution.py:21
  166.3 6.8 %collective-permute-start.24 = (f32[1024]{0:T(1024)S(1)}, f32[1024]{0:T(1024)S(1)}, u32[]{:S(2)}, u32[]{:S(2)}) collective-permute-start(f32[1024]{0:T(1024)S(1)} %bitcast.197), channel_id=1, source_target_pairs={{28,0},{0,4},{4,8},{8,12},{12,16},{16,20},{20,24},{24,28},{29,1},{... | collective-permute-start | bytes 12296 | tf_op jit(solution)/shard_map/ppermute | solution.py:29
  166.4 6.7 %collective-permute-start.25 = (f32[1024]{0:T(1024)S(1)}, f32[1024]{0:T(1024)S(1)}, u32[]{:S(2)}, u32[]{:S(2)}) collective-permute-start(f32[1024]{0:T(1024)S(1)} %bitcast.200), channel_id=1, source_target_pairs={{4,0},{8,4},{12,8},{16,12},{20,16},{24,20},{28,24},{0,28},{5,1},{9... | collective-permute-start | bytes 12296 | tf_op jit(solution)/shard_map/ppermute | solution.py:29
  184.6 13.0 %collective-permute-start.30 = (f32[1,256]{1,0:T(1,128)S(1)}, f32[1,256]{1,0:T(1,128)S(1)}, u32[]{:S(2)}, u32[]{:S(2)}) collective-permute-start(f32[1,256]{1,0:T(1,128)S(1)} %bitcast.210), channel_id=1, source_target_pairs={{0,1},{1,2},{2,3},{4,5},{5,6},{6,7},{8,9},{9,10},{10,11},{12,13},{... | collective-permute-start | bytes 3080 | tf_op jit(solution)/shard_map/ppermute | solution.py:20
  189.7 7.7 %collective-permute-start.31 = (f32[1,256]{1,0:T(1,128)S(1)}, f32[1,256]{1,0:T(1,128)S(1)}, u32[]{:S(2)}, u32[]{:S(2)}) collective-permute-start(f32[1,256]{1,0:T(1,128)S(1)} %bitcast.215), channel_id=1, source_target_pairs={{1,0},{2,1},{3,2},{5,4},{6,5},{7,6},{9,8},{10,9},{11,10},{13,12},{... | collective-permute-start | bytes 3080 | tf_op jit(solution)/shard_map/ppermute | solution.py:21
  191.0 6.7 %collective-permute-start.28 = (f32[1024]{0:T(1024)S(1)}, f32[1024]{0:T(1024)S(1)}, u32[]{:S(2)}, u32[]{:S(2)}) collective-permute-start(f32[1024]{0:T(1024)S(1)} %bitcast.187), channel_id=1, source_target_pairs={{28,0},{0,4},{4,8},{8,12},{12,16},{16,20},{20,24},{24,28},{29,1},{... | collective-permute-start | bytes 12296 | tf_op jit(solution)/shard_map/ppermute | solution.py:29
  191.1 6.7 %collective-permute-start.29 = (f32[1024]{0:T(1024)S(1)}, f32[1024]{0:T(1024)S(1)}, u32[]{:S(2)}, u32[]{:S(2)}) collective-permute-start(f32[1024]{0:T(1024)S(1)} %bitcast.188), channel_id=1, source_target_pairs={{4,0},{8,4},{12,8},{16,12},{20,16},{24,20},{28,24},{0,28},{5,1},{9... | collective-permute-start | bytes 12296 | tf_op jit(solution)/shard_map/ppermute | solution.py:29
  209.4 56.5 %copy-start.9 = (s32[1024]{0:T(1024)S(1)}, s32[1024]{0:T(1024)}, u32[]{:S(2)}) copy-start(s32[1024]{0:T(1024)} %param.31) | copy-start | bytes 12292
  258.1 5.3 %collective-permute-start.32 = (f32[256,128]{1,0:T(8,128)}, f32[256,128]{1,0:T(8,128)S(1)}, u32[]{:S(2)}, u32[]{:S(2)}) collective-permute-start(f32[256,128]{1,0:T(8,128)} %reduce-scatter.2.cloned.1.call-done), channel_id=1, source_target_pairs={{0,4},{4,0},{8,12},{12,8},{16,20},{20,16},{24,28},{28,24},{1,5},{5... | collective-permute-start | bytes 393224 | tf_op jit(solution)/shard_map/ppermute | solution.py:162
  264.4 5.0 %collective-permute-start.33 = (f32[256,128]{1,0:T(8,128)S(1)}, f32[256,128]{1,0:T(8,128)S(1)}, u32[]{:S(2)}, u32[]{:S(2)}) collective-permute-start(f32[256,128]{1,0:T(8,128)S(1)} %add.365), channel_id=1, source_target_pairs={{0,8},{4,12},{8,0},{12,4},{16,24},{20,28},{24,16},{28,20},{1,9},{5... | collective-permute-start | bytes 393224 | tf_op jit(solution)/shard_map/ppermute | solution.py:162
  269.4 7.3 %collective-permute-start.34 = (f32[256,128]{1,0:T(8,128)S(1)}, f32[256,128]{1,0:T(8,128)S(1)}, u32[]{:S(2)}, u32[]{:S(2)}) collective-permute-start(f32[256,128]{1,0:T(8,128)S(1)} %add.366), channel_id=1, source_target_pairs={{0,16},{4,20},{8,24},{12,28},{16,0},{20,4},{24,8},{28,12},{1,17},{... | collective-permute-start | bytes 393224 | tf_op jit(solution)/shard_map/ppermute | solution.py:162
  276.8 6.9 %copy-start.6 = (f32[256,128]{1,0:T(8,128)}, f32[256,128]{1,0:T(8,128)S(1)}, u32[]{:S(2)}) copy-start(f32[256,128]{1,0:T(8,128)S(1)} %add.367) | copy-start | bytes 393220
  (4 other events, 16.0 us)
Sparse Core Ops, SparseCore 0:
  232.4 25.7 reduce-scatter.1
